TPU v7x, 32 devices: a whole 2x2x4 slice. The times are simulated.
32 devices in a mesh: expert: 4 (over y, core), context: 2 (over x), dp: 4 (over z).
Axes of the slice: x: 2, y: 2, z: 4, core: 2. Of those that a mesh axis runs over, the one named last changes fastest.
Arguments:
- layer_input: bfloat16 [4, 1024, 2048], P('dp', ('expert', 'context')), may hold values from -6 to 6
- output_grad: bfloat16 [4, 1024, 2048], P('dp', ('expert', 'context')), may hold values from -6 to 6
- lengths: int32 [4], P('dp'), may hold values from 256 to 1024, as said below
- attn_routes: int32 [4, 1024, 2], P('dp', ('expert', 'context')), may hold values from 0 to 3, all different within a row; in each aligned block of 128 rows (0 to 127, 128 to 255, ..., all dimensions but the last counted through in order) at most 68 rows name the same one
- ffn_routes: int32 [4, 1024, 2], P('dp', ('expert', 'context')), may hold values from 0 to 3, all different within a row; in each aligned block of 128 rows (0 to 127, 128 to 255, ..., all dimensions but the last counted through in order) at most 68 rows name the same one
- norm1_gain: float32 [2048], replicated, may hold values from 0.1 to 1.9
- norm2_gain: float32 [2048], replicated, may hold values from 0.1 to 1.9
- attn_router: bfloat16 [2048, 4], replicated, may hold values from -0.125 to 0.125
- ffn_router: bfloat16 [2048, 4], replicated, may hold values from -0.125 to 0.125
- w_kv: bfloat16 [2048, 4096], P(('context', 'dp')), may hold values from -0.125 to 0.125
- w_query: bfloat16 [4, 2048, 2048], P('expert', ('context', 'dp')), may hold values from -0.125 to 0.125
- w_out: bfloat16 [4, 2048, 2048], P('expert', ('context', 'dp')), may hold values from -2 to 2
- w_in: bfloat16 [4, 11264, 2048], P('expert', ('context', 'dp')), may hold values from -0.125 to 0.125
- w_down: bfloat16 [4, 5632, 2048], P('expert', ('context', 'dp')), may hold values from -0.078125 to 0.078125
Outputs:
- layer_output: bfloat16 [4, 1024, 2048], P('dp', ('expert', 'context'))
- input_grad: float32 [4, 1024, 2048], P('dp', ('expert', 'context'))
- grad_norm1_gain: float32 [2048], replicated
- grad_norm2_gain: float32 [2048], replicated
- grad_attn_router: float32 [2048, 4], replicated
- grad_ffn_router: float32 [2048, 4], replicated
- grad_w_kv: float32 [2048, 4096], P(('context', 'dp'))
- grad_w_query: float32 [4, 2048, 2048], P('expert', ('context', 'dp'))
- grad_w_out: float32 [4, 2048, 2048], P('expert', ('context', 'dp'))
- grad_w_in: float32 [4, 11264, 2048], P('expert', ('context', 'dp'))
- grad_w_down: float32 [4, 5632, 2048], P('expert', ('context', 'dp'))
Inputs may be any that keep to these rules, and one draw needn't show every extreme that they name: Slot s holds one sequence at positions 0 to lengths[s] - 1; the rest is padding. `attn_routes`: the two experts of a position differ; among the 128 positions of one device no expert is named by more than 68. `ffn_routes`: the two experts of a position differ; among the 128 positions of one device no expert is named by more than 68.
All inputs are finite; a program needn't handle non-finite values.
Results may differ from a plain program's by a relative error of at most 0.033.
Values may be sent and summed in bfloat16 or wider, within the bound.
A program may use at most 384 MiB of HBM per device.

v0:
```python
import math

import jax
import jax.numpy as jnp
from jax import lax
from jax.sharding import PartitionSpec as P

HEADS = 16
HEAD_DIM = 128
FF = 5632
TOP = 2
QD = 2048


EPSILON = 1e-06
PRECISE = lax.Precision.HIGHEST


def rms_scale(value):
    return lax.rsqrt(jnp.mean(value * value, axis=-1, keepdims=True) + EPSILON)


def norm_back(value, scale, gain, grad_normed):
    weighted = grad_normed * gain
    d_gain = jnp.sum(grad_normed * value * scale, axis=0)
    d_value = scale * weighted - value * scale**3 * jnp.mean(
        weighted * value, axis=-1, keepdims=True
    )
    return (d_value, d_gain)


def weight_fold(left_rows, weight):
    return jnp.dot(
        left_rows,
        lax.all_gather(weight, ("context", "dp"), axis=0, tiled=True),
        preferred_element_type=jnp.float32,
    )


def weight_back(gradient, weight):
    return lax.dot_general(
        gradient,
        lax.all_gather(weight, ("context", "dp"), axis=0, tiled=True),
        (((1,), (1,)), ((), ())),
        preferred_element_type=jnp.float32,
    )


def weight_grad(left_rows, gradient):
    return lax.psum_scatter(
        lax.dot_general(
            left_rows, gradient, (((0,), (0,)), ((), ())), preferred_element_type=jnp.float32
        ).astype(jnp.bfloat16),
        ("context", "dp"),
        scatter_dimension=0,
        tiled=True,
    ).astype(jnp.float32)


def unit_forward(left_rows, weight):
    return lax.dot_general(
        left_rows,
        lax.all_gather(weight, ("context", "dp"), axis=0, tiled=True),
        (((1,), (1,)), ((), ())),
        preferred_element_type=jnp.float32,
    )


def unit_backward(gradient, weight):
    return jnp.dot(
        gradient,
        lax.all_gather(weight, ("context", "dp"), axis=0, tiled=True),
        preferred_element_type=jnp.float32,
    )


def unit_grad(gradient, left_rows):
    return lax.psum_scatter(
        lax.dot_general(
            gradient, left_rows, (((0,), (0,)), ((), ())), preferred_element_type=jnp.float32
        ).astype(jnp.bfloat16),
        ("context", "dp"),
        scatter_dimension=0,
        tiled=True,
    ).astype(jnp.float32)


def to_owner(slot_rows):
    return lax.all_to_all(slot_rows, "expert", split_axis=0, concat_axis=0, tiled=True)


def to_home(slot_rows):
    return lax.all_to_all(slot_rows, "expert", split_axis=0, concat_axis=0, tiled=True)


def pair_gates(logits, routes, live, experts):
    picked = (routes[:, :, None] == jnp.arange(experts, dtype=jnp.int32)[None, None, :]).astype(
        jnp.float32
    )
    chosen = jnp.sum(picked * logits[:, None, :], axis=-1)
    highest = jnp.max(chosen, axis=-1, keepdims=True)
    exponent = jnp.exp(chosen - highest)
    return (exponent / jnp.sum(exponent, axis=-1, keepdims=True) * live[:, None], picked)


def logit_grad(shares, picked, pair_grad):
    mean_grad = jnp.sum(shares * pair_grad, axis=-1, keepdims=True)
    return jnp.sum((shares * (pair_grad - mean_grad))[:, :, None] * picked, axis=1)


def route_table(routes, live_int, experts, capacity):
    owners = (routes[:, :, None] == jnp.arange(experts, dtype=jnp.int32)[None, None, :]).astype(
        jnp.int32
    )
    owners = owners * live_int[:, None, None]
    used_slots = jnp.sum(owners, axis=1)
    before = jnp.cumsum(used_slots, axis=0) - used_slots
    slot_rank = jnp.sum(before[:, None, :] * owners, axis=-1)
    target = routes * capacity + slot_rank
    slot_hits = (
        target[:, :, None] == jnp.arange(experts * capacity, dtype=jnp.int32)[None, None, :]
    ).astype(jnp.int32)
    return slot_hits * live_int[:, None, None]


def dispatch(table_low, token_rows, experts, capacity):
    sent = jnp.einsum("tkr,td->rd", table_low, token_rows, preferred_element_type=jnp.float32)
    return sent.astype(jnp.bfloat16).reshape(experts, capacity, token_rows.shape[1])


def collect_pairs(table_low, received):
    flat = received.reshape(-1, received.shape[-1])
    return jnp.einsum("tkr,rd->tkd", table_low, flat, preferred_element_type=jnp.float32)


def collect_sum(table_low, received):
    flat = received.reshape(-1, received.shape[-1])
    return jnp.einsum("tkr,rd->td", table_low, flat, preferred_element_type=jnp.float32)


def spread_back(table_int, shares, gradient, experts, capacity):
    weighted = shares[:, :, None] * gradient[:, None, :]
    sent = jnp.einsum("tkr,tkd->rd", table_int.astype(jnp.float32), weighted, precision=PRECISE)
    return sent.astype(jnp.bfloat16).reshape(experts, capacity, gradient.shape[1])


def masked_scores(query_heads, key_heads, query_pos, key_pos):
    scores = jnp.einsum(
        "rhd,khd->hrk", query_heads, key_heads, preferred_element_type=jnp.float32
    ) * HEAD_DIM ** (-0.5)
    return (scores, key_pos[None, None, :] <= query_pos[None, :, None])


def key_scan(shard_piece, block_step, carried):
    piece_len = shard_piece.shape[0]
    block_len = math.gcd(piece_len, 512)
    blocks = shard_piece.reshape(piece_len // block_len, block_len, shard_piece.shape[1])
    firsts = jnp.arange(piece_len // block_len, dtype=jnp.int32) * block_len

    def key_one_block(carry_in, element):
        block_rows, first_key = element
        key_heads = block_rows[:, :QD].reshape(block_len, HEADS, HEAD_DIM)
        value_heads = block_rows[:, QD:].reshape(block_len, HEADS, HEAD_DIM)
        key_pos = first_key + jnp.arange(block_len, dtype=jnp.int32)
        return (block_step(carry_in, key_heads, value_heads, key_pos), None)

    carried, _ = lax.scan(key_one_block, carried, (blocks, firsts))
    return carried


def key_fold(kv_rows, block_step, zeros_init):
    return key_scan(
        lax.all_gather(kv_rows, ("expert", "context"), axis=0, tiled=True), block_step, zeros_init
    )


def on_device(
    layer_input,
    output_grad,
    lengths,
    attn_routes,
    ffn_routes,
    norm1_gain,
    norm2_gain,
    attn_router,
    ffn_router,
    w_kv,
    w_query,
    w_out,
    w_in,
    w_down,
):
    tokens = layer_input.shape[1]
    width = layer_input.shape[2]
    experts = lax.axis_size("expert")
    capacity = tokens * TOP // experts + tokens // 32
    row_count = experts * capacity
    position = lax.axis_index(("expert", "context")) * tokens + jnp.arange(tokens, dtype=jnp.int32)
    live_int = (position < lengths[0]).astype(jnp.int32)
    live = live_int.astype(jnp.float32)
    x_float = layer_input[0].astype(jnp.float32)
    scale_one = rms_scale(x_float)
    normed_one = (x_float * scale_one * norm1_gain).astype(jnp.bfloat16)
    kv_rows = weight_fold(normed_one, w_kv).astype(jnp.bfloat16)
    shares_a, picked_a = pair_gates(
        jnp.dot(normed_one, attn_router, preferred_element_type=jnp.float32),
        attn_routes[0],
        live,
        experts,
    )
    table_a = route_table(attn_routes[0], live_int, experts, capacity)
    low_table_a = table_a.astype(jnp.bfloat16)
    send_rows = dispatch(low_table_a, normed_one, experts, capacity)
    send_pos = jnp.einsum("tkr,t->r", table_a, position).reshape(experts, capacity)
    got_rows, got_pos = (
        lax.all_to_all(send_rows, "expert", split_axis=0, concat_axis=0, tiled=True),
        lax.all_to_all(send_pos, "expert", split_axis=0, concat_axis=0, tiled=True),
    )
    routed_one = got_rows.reshape(row_count, width)
    slot_pos = got_pos.reshape(row_count)
    query = weight_fold(routed_one, w_query[0]).astype(jnp.bfloat16)
    query_heads = query.reshape(row_count, HEADS, HEAD_DIM)

    def stat_step(carry_in, key_heads, value_heads, key_pos):
        highest, running = carry_in
        scores, allowed = masked_scores(query_heads, key_heads, slot_pos, key_pos)
        new_high = jnp.maximum(highest, jnp.max(jnp.where(allowed, scores, -1e30), axis=-1))
        running = running * jnp.exp(highest - new_high) + jnp.sum(
            jnp.where(allowed, jnp.exp(scores - new_high[:, :, None]), 0.0), axis=-1
        )
        return (new_high, running)

    highest, running = key_fold(
        kv_rows,
        stat_step,
        (
            jnp.full((HEADS, row_count), -1e30, jnp.float32),
            jnp.zeros((HEADS, row_count), jnp.float32),
        ),
    )
    log_norm = highest + jnp.log(running)

    def value_step(carry_in, key_heads, value_heads, key_pos):
        scores, allowed = masked_scores(query_heads, key_heads, slot_pos, key_pos)
        probabilities = jnp.where(allowed, jnp.exp(scores - log_norm[:, :, None]), 0.0).astype(
            jnp.bfloat16
        )
        return carry_in + jnp.einsum(
            "hrk,khd->rhd", probabilities, value_heads, preferred_element_type=jnp.float32
        )

    attended = key_fold(kv_rows, value_step, jnp.zeros((row_count, HEADS, HEAD_DIM), jnp.float32))
    attended = attended.reshape(row_count, QD).astype(jnp.bfloat16)
    branch_rows = weight_fold(attended, w_out[0]).astype(jnp.bfloat16)
    branch_back = to_home(branch_rows.reshape(experts, capacity, width))
    branch_pairs = collect_pairs(low_table_a, branch_back)
    residual_one = x_float + jnp.sum(shares_a[:, :, None] * branch_pairs, axis=1)
    scale_two = rms_scale(residual_one)
    normed_two = (residual_one * scale_two * norm2_gain).astype(jnp.bfloat16)
    shares_f, picked_f = pair_gates(
        jnp.dot(normed_two, ffn_router, preferred_element_type=jnp.float32),
        ffn_routes[0],
        live,
        experts,
    )
    table_f = route_table(ffn_routes[0], live_int, experts, capacity)
    low_table_f = table_f.astype(jnp.bfloat16)
    routed_two = to_owner(dispatch(low_table_f, normed_two, experts, capacity)).reshape(
        row_count, width
    )
    both = unit_forward(routed_two, w_in[0])
    hidden = (jax.nn.silu(both[:, :FF]) * both[:, FF:]).astype(jnp.bfloat16)
    down_rows = weight_fold(hidden, w_down[0]).astype(jnp.bfloat16)
    down_back = to_home(down_rows.reshape(experts, capacity, width))
    down_pairs = collect_pairs(low_table_f, down_back)
    mixed = jnp.sum(shares_f[:, :, None] * down_pairs, axis=1)
    layer_output = (live[:, None] * (residual_one + mixed)).astype(jnp.bfloat16)
    grad_out = output_grad[0].astype(jnp.float32) * live[:, None]
    pair_grad_f = jnp.sum(grad_out[:, None, :] * down_pairs, axis=-1)
    d_down = to_owner(spread_back(table_f, shares_f, grad_out, experts, capacity)).reshape(
        row_count, width
    )
    d_hidden = weight_back(d_down, w_down[0])
    gate_part = both[:, :FF]
    up_part = both[:, FF:]
    sigmoid_gate = jax.nn.sigmoid(gate_part)
    d_gate = d_hidden * up_part * sigmoid_gate * (1.0 + gate_part * (1.0 - sigmoid_gate))
    d_up = d_hidden * gate_part * sigmoid_gate
    d_gate_up = jnp.concatenate([d_gate, d_up], axis=1).astype(jnp.bfloat16)
    d_routed_two = unit_backward(d_gate_up, w_in[0]).astype(jnp.bfloat16)
    grad_w_in = unit_grad(d_gate_up, routed_two)
    grad_w_down = weight_grad(hidden, d_down)
    d_copy_two = to_home(d_routed_two.reshape(experts, capacity, width))
    dlog_f = logit_grad(shares_f, picked_f, pair_grad_f)
    d_normed_two = collect_sum(low_table_f, d_copy_two) + jnp.dot(
        dlog_f, ffn_router.astype(jnp.float32).T, precision=PRECISE
    )
    local_ffn_router = jnp.dot(normed_two.astype(jnp.float32).T, dlog_f, precision=PRECISE)
    d_mid, local_gain_two = norm_back(residual_one, scale_two, norm2_gain, d_normed_two)
    d_residual = grad_out + d_mid
    pair_grad_a = jnp.sum(d_residual[:, None, :] * branch_pairs, axis=-1)
    d_branch = to_owner(spread_back(table_a, shares_a, d_residual, experts, capacity)).reshape(
        row_count, width
    )
    d_attended = weight_back(d_branch, w_out[0]).astype(jnp.bfloat16)
    grad_w_out = weight_grad(attended, d_branch)
    delta_rows = jnp.sum(
        (d_attended.astype(jnp.float32) * attended.astype(jnp.float32)).reshape(
            row_count, HEADS, HEAD_DIM
        ),
        axis=-1,
    )
    delta_sum = delta_rows.T
    d_attended_heads = d_attended.reshape(row_count, HEADS, HEAD_DIM)

    def query_grad_step(carry_in, key_heads, value_heads, key_pos):
        scores, allowed = masked_scores(query_heads, key_heads, slot_pos, key_pos)
        probabilities = jnp.where(allowed, jnp.exp(scores - log_norm[:, :, None]), 0.0)
        d_prob = jnp.einsum(
            "rhd,khd->hrk", d_attended_heads, value_heads, preferred_element_type=jnp.float32
        )
        d_scores = (probabilities * (d_prob - delta_sum[:, :, None])).astype(jnp.bfloat16)
        return carry_in + jnp.einsum(
            "hrk,khd->rhd", d_scores, key_heads, preferred_element_type=jnp.float32
        )

    d_query_sum = key_fold(
        kv_rows, query_grad_step, jnp.zeros((row_count, HEADS, HEAD_DIM), jnp.float32)
    )
    d_query = (d_query_sum * HEAD_DIM ** (-0.5)).reshape(row_count, QD).astype(jnp.bfloat16)
    d_routed_one = weight_back(d_query, w_query[0]).astype(jnp.bfloat16)
    grad_w_query = weight_grad(routed_one, d_query)
    d_copy_one = to_home(d_routed_one.reshape(experts, capacity, width))
    own_keys = kv_rows[:, :QD].reshape(tokens, HEADS, HEAD_DIM)
    own_values = kv_rows[:, QD:].reshape(tokens, HEADS, HEAD_DIM)
    zeros_heads = jnp.zeros((tokens, HEADS, HEAD_DIM), jnp.float32)
    carried = (zeros_heads, zeros_heads)
    shard_piece = (
        lax.all_gather(query, ("expert", "context"), axis=0, tiled=True),
        lax.all_gather(d_attended, ("expert", "context"), axis=0, tiled=True),
        lax.all_gather(
            log_norm.T.astype(jnp.bfloat16), ("expert", "context"), axis=0, tiled=True
        ).astype(jnp.float32),
        lax.all_gather(
            delta_rows.astype(jnp.bfloat16), ("expert", "context"), axis=0, tiled=True
        ).astype(jnp.float32),
        lax.all_gather(slot_pos, ("expert", "context"), axis=0, tiled=True),
    )
    piece_len = shard_piece[0].shape[0]
    block_len = math.gcd(piece_len, row_count)

    def body_one_block(carry_in, element):
        query_part, grad_part, norm_part, delta_part, pos_part = element
        query_low = query_part.reshape(block_len, HEADS, HEAD_DIM)
        grad_low = grad_part.reshape(block_len, HEADS, HEAD_DIM)
        scores, allowed = masked_scores(query_low, own_keys, pos_part, position)
        probabilities = jnp.where(allowed, jnp.exp(scores - norm_part.T[:, :, None]), 0.0)
        d_prob = jnp.einsum(
            "rhd,khd->hrk", grad_low, own_values, preferred_element_type=jnp.float32
        )
        d_scores = (probabilities * (d_prob - delta_part.T[:, :, None])).astype(jnp.bfloat16)
        d_keys, d_values = carry_in
        d_keys = d_keys + jnp.einsum(
            "hrk,rhd->khd", d_scores, query_low, preferred_element_type=jnp.float32
        )
        d_values = d_values + jnp.einsum(
            "hrk,rhd->khd",
            probabilities.astype(jnp.bfloat16),
            grad_low,
            preferred_element_type=jnp.float32,
        )
        return ((d_keys, d_values), None)

    shaped = tuple(
        (
            member.reshape((piece_len // block_len, block_len) + member.shape[1:])
            for member in shard_piece
        )
    )
    carried, _ = lax.scan(body_one_block, carried, shaped)
    d_keys, d_values = carried
    d_kv = jnp.concatenate(
        [d_keys.reshape(tokens, QD) * HEAD_DIM ** (-0.5), d_values.reshape(tokens, QD)], axis=1
    ).astype(jnp.bfloat16)
    grad_w_kv = lax.psum(weight_grad(normed_one, d_kv).astype(jnp.bfloat16), "expert").astype(
        jnp.float32
    )
    dlog_a = logit_grad(shares_a, picked_a, pair_grad_a)
    d_normed_one = (
        collect_sum(low_table_a, d_copy_one)
        + weight_back(d_kv, w_kv)
        + jnp.dot(dlog_a, attn_router.astype(jnp.float32).T, precision=PRECISE)
    )
    local_attn_router = jnp.dot(normed_one.astype(jnp.float32).T, dlog_a, precision=PRECISE)
    d_first, local_gain_one = norm_back(x_float, scale_one, norm1_gain, d_normed_one)
    input_grad = d_residual + d_first
    gain_one_sum, gain_two_sum, router_a_sum, router_f_sum = lax.psum(
        (local_gain_one, local_gain_two, local_attn_router, local_ffn_router),
        ("expert", "context", "dp"),
    )
    return (
        layer_output[None],
        input_grad[None],
        gain_one_sum,
        gain_two_sum,
        router_a_sum,
        router_f_sum,
        grad_w_kv,
        grad_w_query[None],
        grad_w_out[None],
        grad_w_in[None],
        grad_w_down[None],
    )


def solution(mesh):
    placed = (
        P("dp", ("expert", "context"), None),
        P("dp", ("expert", "context"), None),
        P("dp"),
        P("dp", ("expert", "context"), None),
        P("dp", ("expert", "context"), None),
        P(),
        P(),
        P(),
        P(),
        P(("context", "dp"), None),
        P("expert", ("context", "dp"), None),
        P("expert", ("context", "dp"), None),
        P("expert", ("context", "dp"), None),
        P("expert", ("context", "dp"), None),
    )
    return jax.shard_map(
        on_device,
        mesh=mesh,
        in_specs=placed,
        out_specs=(
            P("dp", ("expert", "context"), None),
            P("dp", ("expert", "context"), None),
            P(),
            P(),
            P(),
            P(),
            P(("context", "dp"), None),
            P("expert", ("context", "dp"), None),
            P("expert", ("context", "dp"), None),
            P("expert", ("context", "dp"), None),
            P("expert", ("context", "dp"), None),
        ),
        check_vma=False,
    )
```

profile of v0, /device:TPU:8, one launch (start us, length us, event | category | flops | bytes accessed | tf_op | source)
XLA Modules:
  0.0 4069.2 jit_solution(7593083386185275639)
XLA Ops:
  9.5 227.3 %all-gather.15.cloned.1.call-done = bf16[2048,4096]{1,0:T(8,128)(2,1)} async-done(((bf16[256,4096]{1,0:T(8,128)(2,1)}), bf16[2048,4096]{1,0:T(8,128)(2,1)}) %all-gather.15.cloned.1.call-update) | async-done | bytes 16777232 | tf_op jit(solution)/shard_map/all_gather | solution.py:35
  236.8 9.2 convolution_convert_fusion.5
  261.9 15.2 all-to-all-done.1
  277.4 84.2 %all-gather.23.cloned.1.call-done = bf16[1,2048,2048]{2,1,0:T(8,128)(2,1)} async-done(((bf16[1,256,2048]{2,1,0:T(8,128)(2,1)}), bf16[1,2048,2048]{2,1,0:T(8,128)(2,1)}) %all-gather.23.cloned.1.call-update) | async-done | bytes 8388624 | tf_op jit(solution)/shard_map/all_gather | solution.py:35
  361.6 5.8 fusion.76
  367.7 50.7 %all-gather.17.cloned.1.call-done = bf16[1024,4096]{1,0:T(8,128)(2,1)} async-done(((bf16[128,4096]{1,0:T(8,128)(2,1)}), bf16[1024,4096]{1,0:T(8,128)(2,1)}) %all-gather.17.cloned.1.call-update) | async-done | bytes 8388624 | tf_op jit(solution)/shard_map/all_gather | solution.py:173
  418.4 12.1 copy.124
  430.5 29.1 while.52
  434.5 5.3 fusion.278
  439.8 5.2 fusion.279
  449.0 5.3 fusion.278
  454.4 5.2 fusion.279
  460.2 27.0 while.53
  466.4 6.7 bitcast_add_fusion.6
  479.4 7.4 bitcast_add_fusion.6
  487.3 55.7 %all-gather.25.cloned.1.call-done = bf16[1,2048,2048]{2,1,0:T(8,128)(2,1)} async-done(((bf16[1,256,2048]{2,1,0:T(8,128)(2,1)}), bf16[1,2048,2048]{2,1,0:T(8,128)(2,1)}) %all-gather.25.cloned.1.call-update) | async-done | bytes 8388624 | tf_op jit(solution)/shard_map/all_gather | solution.py:35
  543.0 7.5 fusion.82
  557.9 15.2 all-to-all-done.2
  592.7 10.2 all-to-all-done.3
  610.3 12.8 all-to-all-done.5
  625.3 792.8 %all-gather.27.cloned.1.call-done = bf16[1,11264,2048]{2,1,0:T(8,128)(2,1)} async-done(((bf16[1,1408,2048]{2,1,0:T(8,128)(2,1)}), bf16[1,11264,2048]{2,1,0:T(8,128)(2,1)}) %all-gather.27.cloned.1.call-update) | async-done | bytes 46137360 | tf_op jit(solution)/shard_map/all_gather | solution.py:63
  1418.1 23.4 fusion.57
  1441.5 420.3 %all-gather.29.cloned.1.call-done = bf16[1,5632,2048]{2,1,0:T(8,128)(2,1)} async-done(((bf16[1,704,2048]{2,1,0:T(8,128)(2,1)}), bf16[1,5632,2048]{2,1,0:T(8,128)(2,1)}) %all-gather.29.cloned.1.call-update) | async-done | bytes 23068688 | tf_op jit(solution)/shard_map/all_gather | solution.py:35
  1861.8 19.1 multiply_convert_fusion.2
  1882.7 12.3 fusion.71
  1901.5 21.8 fusion.88
  1925.4 5.0 all-to-all-done.4
  1937.1 13.5 all-to-all-done.6
  1962.0 19.0 all_to_all.52
  1982.4 7.3 fusion.85
  1992.6 24.7 all-reduce
  2018.7 17.3 all-gather.4
  2041.1 16.0 all-gather.5
  2057.9 117.6 %while.51 = (s32[]{:T(128)}, f32[128,16,128]{0,2,1:T(8,128)}, f32[128,16,128]{0,2,1:T(8,128)}, bf16[8,272,2048]{2,1,0:T(8,128)(2,1)}, s32[8,272]{1,0:T(8,128)S(1...) while((s32[]{:T(128)}, f32[128,16,128]{0,2,1:T(8,128)}, ...), condition=%wide.region_33.34_spmd.clone, body=%wide.region_32.33_spmd.clone.sunk | while | flops 577079424 | bytes 25527648 | solution.py:380
  2063.5 4.8 fusion.274
  2077.7 5.0 fusion.274
  2092.4 5.0 fusion.274
  2107.1 5.0 fusion.274
  2121.8 5.0 fusion.274
  2136.6 5.0 fusion.274
  2151.3 5.0 fusion.274
  2166.0 5.0 fusion.274
  2177.2 8.9 convolution_convert_fusion.2
  2188.6 36.5 while.54
  2192.8 4.9 fusion.293
  2199.1 7.6 bitcast_add_fusion.7
  2210.8 4.9 fusion.293
  2217.0 8.1 bitcast_add_fusion.7
  2225.1 10.1 convolution_convert_fusion.4
  2237.1 6.8 convolution_convert_fusion.3
  2245.1 17.5 convolution_convert_fusion.1
  2262.7 202.9 %reduce-scatter.8.cloned.1.call-done = bf16[256,4096]{1,0:T(8,128)(2,1)} async-done(((bf16[2048,4096]{1,0:T(8,128)(2,1)}), bf16[256,4096]{1,0:T(8,128)(2,1)}) %reduce-scatter.8.cloned.1.call-update) | async-done | bytes 2097168 | tf_op jit(solution)/shard_map/reduce_scatter | solution.py:50
  2465.6 32.0 convolution_convert_fusion
  2501.8 7.0 fusion.79
  2519.1 12.2 all-to-all-done.8
  2533.5 12.6 fusion.125
  2551.1 65.2 %reduce-scatter.10.cloned.1.call-done = bf16[256,2048]{1,0:T(8,128)(2,1)} async-done(((bf16[2048,2048]{1,0:T(8,128)(2,1)}), bf16[256,2048]{1,0:T(8,128)(2,1)}) %reduce-scatter.10.cloned.1.call-update) | async-done | bytes 1048592 | tf_op jit(solution)/shard_map/reduce_scatter | solution.py:50
  2619.0 147.4 %reduce-scatter.12.cloned.1.call-done = bf16[256,2048]{1,0:T(8,128)(2,1)} async-done(((bf16[2048,2048]{1,0:T(8,128)(2,1)}), bf16[256,2048]{1,0:T(8,128)(2,1)}) %reduce-scatter.12.cloned.1.call-update) | async-done | bytes 1048592 | tf_op jit(solution)/shard_map/reduce_scatter | solution.py:50
  2769.2 372.6 %reduce-scatter.14.cloned.1.call-done = bf16[704,2048]{1,0:T(8,128)(2,1)} async-done(((bf16[5632,2048]{1,0:T(8,128)(2,1)}), bf16[704,2048]{1,0:T(8,128)(2,1)}) %reduce-scatter.14.cloned.1.call-update) | async-done | bytes 2883600 | tf_op jit(solution)/shard_map/reduce_scatter | solution.py:50
  3141.8 5.1 bitcast_convert_fusion.1
  3146.9 49.3 %all-reduce.6.cloned.1.call-done = bf16[256,4096]{1,0:T(8,128)(2,1)} async-done(((bf16[256,4096]{1,0:T(8,128)(2,1)}), bf16[256,4096]{1,0:T(8,128)(2,1)}) %all-reduce.6.cloned.1.call-update) | async-done | bytes 2097168 | tf_op jit(solution)/shard_map/psum | solution.py:385
  3200.4 723.6 %reduce-scatter.16.cloned.1.call-done = bf16[1408,2048]{1,0:T(8,128)(2,1)} async-done(((bf16[11264,2048]{1,0:T(8,128)(2,1)}), bf16[1408,2048]{1,0:T(8,128)(2,1)}) %reduce-scatter.16.cloned.1.call-update) | async-done | bytes 5767184
  3923.9 8.7 bitcast_convert_fusion
  3932.6 124.5 %all-reduce.8.cloned.1.call-done = (f32[2048]{0:T(1024)}, f32[2048]{0:T(1024)}, f32[2048,4]{0,1:T(4,128)}, f32[2048,4]{0,1:T(4,128)}) async-done(((f32[2048]{0:T(1024)}, f32[2048]{0:T(1024)}, f32[2048,4]{0,1:T(4,128)}, f32[2048,4]{0,1:T(4,128)}), (f32[2048]{0:T(1024)}, f32[2048]{0:T(1024)}, f32[2048,4]{0,1:T(4,128)}, f32[2048,4]{0,1:T(4,128)})) %all-reduce.8.cloned.1.call-update) | async-done | bytes 81936 | tf_op jit(solution)/shard_map/psum | solution.py:397
  (393 shorter events, 245.7 us)
Async XLA Ops:
  7.2 579.8 %copy-start = (bf16[2048,4]{0,1:T(4,128)(2,1)S(1)}, bf16[2048,4]{0,1:T(4,128)(2,1)}, u32[]{:S(2)}) copy-start(bf16[2048,4]{0,1:T(4,128)(2,1)} %param.30) | copy-start | bytes 49156
  7.2 229.6 %copy-start.31 = (f32[2048]{0:T(1024)S(1)}, f32[2048]{0:T(1024)}, u32[]{:S(2)}) copy-start(f32[2048]{0:T(1024)} %param.27) | copy-start | bytes 24580
  7.2 229.6 %all-gather.15.cloned.1.call-start = ((), (), s32[]{:S(2)}) async-start(), calls=%async_computation.14 | async-start | bytes 18874368 | tf_op jit(solution)/shard_map/all_gather | solution.py:35
  8.0 353.6 %all-gather.23.cloned.1.call-start = ((), (), s32[]{:S(2)}) async-start(), calls=%async_computation.23 | async-start | bytes 9437184 | tf_op jit(solution)/shard_map/all_gather | solution.py:35
  8.7 409.7 %all-gather.17.cloned.1.call-start = ((), (), s32[]{:S(2)}) async-start(), calls=%async_computation.15 | async-start | bytes 9437184 | tf_op jit(solution)/shard_map/all_gather | solution.py:173
  9.5 251.9 %copy-start.47 = (f32[128]{0:T(128)}, f32[128]{0:T(128)S(1)}, u32[]{:S(2)}) copy-start(f32[128]{0:T(128)S(1)} %get-tuple-element.570) | copy-start | bytes 1540
  246.0 297.0 %all-gather.25.cloned.1.call-start = ((), (), s32[]{:S(2)}) async-start(), calls=%async_computation.24 | async-start | bytes 9437184 | tf_op jit(solution)/shard_map/all_gather | solution.py:35
  246.6 1171.5 %all-gather.27.cloned.1.call-start = ((), (), s32[]{:S(2)}) async-start(), calls=%async_computation.25 | async-start | bytes 51904512 | tf_op jit(solution)/shard_map/all_gather | solution.py:63
  247.2 1614.6 %all-gather.29.cloned.1.call-start = ((), (), s32[]{:S(2)}) async-start(), calls=%async_computation.26 | async-start | bytes 25952256 | tf_op jit(solution)/shard_map/all_gather | solution.py:35
  248.4 1709.7 %copy-start.39 = (f32[128]{0:T(128)}, f32[128]{0:T(128)S(1)}, u32[]{:S(2)}) copy-start(f32[128]{0:T(128)S(1)} %get-tuple-element.552) | copy-start | bytes 1540
  250.6 6.9 all-to-all-start
  253.9 3.6 copy-start.34
  254.4 6.9 copy-start.54
  257.5 19.9 copy-start.37
  257.5 19.6 all-to-all-start.1
  277.4 90.1 %copy-start.25 = (bf16[272,2048]{1,0:T(8,128)(2,1)}, bf16[272,2048]{1,0:T(8,128)(2,1)S(1)}, u32[]{:S(2)}) copy-start(bf16[272,2048]{1,0:T(8,128)(2,1)S(1)} %reshape.655) | copy-start | bytes 3342340
  367.5 63.0 %copy-start.19 = (bf16[272,2048]{1,0:T(8,128)(2,1)}, bf16[272,2048]{1,0:T(8,128)(2,1)S(1)}, u32[]{:S(2)}) copy-start(bf16[272,2048]{1,0:T(8,128)(2,1)S(1)} %fusion.76) | copy-start | bytes 3342340
  487.2 55.8 %copy-start.50 = (f32[16,272]{1,0:T(8,128)}, f32[16,272]{1,0:T(8,128)S(1)}, u32[]{:S(2)}) copy-start(f32[16,272]{1,0:T(8,128)S(1)} %get-tuple-element.1157) | copy-start | bytes 52228
  487.3 63.3 %copy-start.2 = (bf16[272,16,128]{2,0,1:T(8,128)(2,1)}, bf16[272,16,128]{2,0,1:T(8,128)(2,1)S(1)}, u32[]{:S(2)}) copy-start(bf16[272,16,128]{2,0,1:T(8,128)(2,1)S(1)} %get-tuple-element.1096) | copy-start | bytes 3342340
  487.3 63.3 %copy-start.62 = (s32[2]{0:T(128)}, s32[2]{0:T(128)S(1)}, u32[]{:S(2)}) copy-start(s32[2]{0:T(128)S(1)} %get-tuple-element.1165) | copy-start | bytes 28
  550.6 7.2 copy-start.23
  552.9 20.2 all-to-all-start.2
  557.2 21.4 copy-start.56
  557.3 21.4 copy-start.58
  575.3 3.6 copy-start.36
  578.6 1379.5 %copy-start.6 = (f32[128,2048]{1,0:T(8,128)}, f32[128,2048]{1,0:T(8,128)S(1)}, u32[]{:S(2)}) copy-start(f32[128,2048]{1,0:T(8,128)S(1)} %get-tuple-element.573) | copy-start | bytes 3145732
  579.1 7.9 copy-start.13
  582.7 20.2 all-to-all-start.3
  602.9 20.2 all-to-all-start.5
  607.2 1450.7 %all-gather.19.cloned.1.call-start = ((), (), s32[]{:S(2)}) async-start(), calls=%async_computation.16 | async-start | bytes 10027008 | tf_op jit(solution)/shard_map/all_gather | solution.py:339
  1897.2 33.2 all-to-all-start.4
  1930.4 20.2 all-to-all-start.6
  1934.7 123.2 %all-gather.21.cloned.1.call-start = ((), (), s32[]{:S(2)}) async-start(), calls=%async_computation.17 | async-start | bytes 10027008 | tf_op jit(solution)/shard_map/all_gather | solution.py:340
  1952.8 3.3 copy-start.20
  1982.4 7.3 copy-start.28
  1982.4 7.4 copy-start.64
  1982.4 9.2 copy-start.38
  1982.4 35.0 copy-start.12
  1989.8 28.9 copy-start.41
  1989.8 475.8 %reduce-scatter.8.cloned.1.call-start = ((), (), s32[]{:S(2)}) async-start(), calls=%async_computation.18 | async-start | bytes 18874368 | tf_op jit(solution)/shard_map/reduce_scatter | solution.py:50
  2017.4 19.2 copy-start.10
  2017.5 19.2 copy-start.21
  2176.9 9.2 copy-start.15
  2177.2 9.0 copy-start.17
  2186.2 430.0 %reduce-scatter.10.cloned.1.call-start = ((), (), s32[]{:S(2)}) async-start(), calls=%async_computation.20 | async-start | bytes 9437184 | tf_op jit(solution)/shard_map/reduce_scatter | solution.py:50
  2235.2 531.2 %reduce-scatter.12.cloned.1.call-start = ((), (), s32[]{:S(2)}) async-start(), calls=%async_computation.21 | async-start | bytes 9437184 | tf_op jit(solution)/shard_map/reduce_scatter | solution.py:50
  2243.9 897.9 %reduce-scatter.14.cloned.1.call-start = ((), (), s32[]{:S(2)}) async-start(), calls=%async_computation.22 | async-start | bytes 25952256 | tf_op jit(solution)/shard_map/reduce_scatter | solution.py:50
  2262.6 203.0 %copy-start.26 = (bf16[272,2048]{1,0:T(8,128)(2,1)S(1)}, bf16[272,2048]{1,0:T(8,128)(2,1)}, u32[]{:S(2)}) copy-start(bf16[272,2048]{1,0:T(8,128)(2,1)} %reshape.660) | copy-start | bytes 3342340
  2262.6 933.6 %all-reduce.6.cloned.1.call-start = ((), (), s32[]{:S(2)}) async-start(), calls=%async_computation.19 | async-start | bytes 4194304 | tf_op jit(solution)/shard_map/psum | solution.py:385
  2465.6 1458.3 %reduce-scatter.16.cloned.1.call-start = ((), (), s32[]{:S(2)}) async-start(), calls=%async_computation.27 | async-start | bytes 51904512
  2497.7 3.1 copy-start.14
  2497.8 4.0 copy-start.61
  2508.7 7.0 copy-start.45
  2508.7 7.0 copy-start.5
  2508.7 7.0 copy-start.33
  2508.7 7.0 copy-start.49
  2511.0 5.8 copy-start.7
  2511.0 20.3 all-to-all-start.8
  2515.4 1541.7 %all-reduce.8.cloned.1.call-start = ((), (), s32[]{:S(2)}) async-start(), calls=%async_computation.28 | async-start | bytes 163840 | tf_op jit(solution)/shard_map/psum | solution.py:397
  2516.8 16.7 copy-start.16
  2519.1 14.4 copy-start.18
  2533.5 12.6 copy-start.35
  2546.1 3.5 copy-start.60
  3923.9 138.5 %copy-start.1 = (bf16[2048,4]{0,1:T(4,128)(2,1)S(1)}, bf16[2048,4]{0,1:T(4,128)(2,1)}, u32[]{:S(2)}) copy-start(bf16[2048,4]{0,1:T(4,128)(2,1)} %param.30) | copy-start | bytes 49156
  (25 other events, 48.2 us)
Sparse Core Ops, SparseCore 0:
  10.2 226.5 all-gather.14
  238.9 122.6 all-gather.22
  364.1 54.2 all-gather.16
  420.4 122.6 all-gather.24
  544.4 873.6 all-gather.26
  1419.5 442.2 all-gather.28
  1863.7 70.3 all-gather.18
  1989.9 57.2 all-gather.20
  2186.3 279.2 reduce-scatter.7
  2469.6 146.5 reduce-scatter.9
  2619.9 146.5 reduce-scatter.11
  2770.2 371.5 reduce-scatter.13
  3144.2 52.0 all-reduce.5
  3200.0 723.8 reduce-scatter.15
  3930.5 126.5 all-reduce.7
where the time goes:
time: 4080 us; the launch traced here: 4070 us
  waiting for transfers between devices  3410 us (84%)
  matrix products  367 us (9%)
  local copies, waits for them, and re-layouts  113 us (3%)
  blocking collectives  77.1 us (2%)
  other arithmetic  54.4 us (1%)
    all_gather x1, waiting for transfers between devices, unit_forward(): lax.all_gather(weight, ('context', 'dp'), axis=0, tiled=True)  793 us
    reduce_scatter x4, waiting for transfers between devices, weight_grad(): lax.psum_scatter(lax.dot_general(left_rows, gradient, (((0,), (0,)), ((),...  788 us
    all_gather x4, waiting for transfers between devices, weight_fold(): lax.all_gather(weight, ('context', 'dp'), axis=0, tiled=True)  788 us
    unnamed x16, waiting for transfers between devices  727 us
    psum x1, waiting for transfers between devices, on_device(): lax.psum((local_gain_one, local_gain_two, local_attn_router, local_ffn_ro...  124 us
  transfers between devices with their start and end apart: 23, of which 21 were waited for; matrix products, arithmetic and copies ran while one was open for 10% of the time, Pallas kernels for 0%

commit v1 on v0

--- a/solution.py
+++ b/solution.py
@@ -3,6 +3,8 @@
 import jax
 import jax.numpy as jnp
 from jax import lax
+from jax.experimental import pallas as pl
+from jax.experimental.pallas import tpu as pltpu
 from jax.sharding import PartitionSpec as P
 
 HEADS = 16
@@ -174,7 +176,7 @@
     )
 
 
-def on_device(
+def gathered_weights(
     layer_input,
     output_grad,
     lengths,
@@ -413,6 +415,596 @@
     )
 
 
+MESH = pl.DeviceIdType.MESH
+EVERY = ("dp", "expert", "context")
+SHARE = ("context", "dp")
+
+class Place:
+    def __init__(self):
+        self.e = lax.axis_index("expert"); self.x = lax.axis_index("context"); self.z = lax.axis_index("dp")
+        self.own = (self.e, self.x)
+        self.c = lax.rem(self.e, 2)
+        self.sib = (self.e + 1 - 2 * self.c, self.x)
+        self.cols = self.columns(self.e, self.x, self.c)
+        self.sib_cols = self.columns(self.sib[0], self.x, 1 - self.c)
+    def columns(self, e, x, c):
+        first = (lax.rem(e + 2 * c, 4), lax.rem(x + 1 - c, 2))
+        second = (lax.rem(e + 2 * (1 - c), 4), lax.rem(x + c, 2))
+        diag = (lax.rem(e + 2, 4), 1 - x)
+        return ((e, x), first, second, diag)
+    def dev(self, col, z=None):
+        return (col[0], col[1], self.z if z is None else z)
+    def block(self, col, z):
+        return z * 8 + col[0] * 2 + col[1]
+
+def greet(pc, sides):
+    barrier = pltpu.get_barrier_semaphore()
+    for col in (pc.sib, pc.cols[1], pc.cols[2]):
+        pl.semaphore_signal(barrier, inc=1, device_id=pc.dev(col), device_id_type=MESH)
+    @pl.when(pc.z > 0)
+    def _():
+        pl.semaphore_signal(barrier, inc=1, device_id=pc.dev(pc.own, pc.z - 1), device_id_type=MESH)
+    @pl.when(pc.z < sides - 1)
+    def _():
+        pl.semaphore_signal(barrier, inc=1, device_id=pc.dev(pc.own, pc.z + 1), device_id_type=MESH)
+    pl.semaphore_wait(barrier, 3 + lax.div(pc.z + sides - 1, sides) + lax.div(2 * sides - 2 - pc.z, sides))
+
+
+def gather_kernel(x_ref, out_ref, loc, zs, zr, fs, fr, ss, sr, bs, br):
+    pc = Place()
+    z = pc.z
+    mine = pltpu.make_async_copy(x_ref, out_ref.at[pc.block(pc.own, z)], loc)
+    mine.start()
+    greet(pc, 4)
+    def rc(src, blk, s, r, dev):
+        return pltpu.make_async_remote_copy(src_ref=src, dst_ref=out_ref.at[blk], send_sem=s, recv_sem=r, device_id=dev, device_id_type=MESH)
+    def hop(col, d, kind):
+        zz = z + d
+        blk = pc.block(pc.cols[col], zz)
+        src = x_ref if (col == 0 and d == 0) else out_ref.at[blk]
+        i = d + 3
+        if kind == "f":
+            return rc(src, blk, fs.at[i], fr.at[i], pc.dev(pc.cols[1]))
+        if kind == "s":
+            return rc(src, blk, ss.at[col, i], sr.at[col, i], pc.dev(pc.cols[2]))
+        return rc(src, blk, bs.at[col, i], br.at[col, i], pc.dev(pc.sib))
+    def zhop(d, up):
+        zz = z + d
+        blk = pc.block(pc.own, zz)
+        src = x_ref if d == 0 else out_ref.at[blk]
+        i = 0 if up else 1
+        return rc(src, blk, zs.at[i, abs(d)], zr.at[i, abs(d)], pc.dev(pc.own, z + 1 if up else z - 1))
+    def ok(d):
+        return (z + d >= 0) & (z + d <= 3)
+    def when(cond, f):
+        if cond is True:
+            f()
+        else:
+            pl.when(cond)(f)
+    def start_z(d):
+        if d <= 0:
+            pl.when(ok(d) & (z < 3))(lambda: zhop(d, True).start())
+        if d >= 0:
+            pl.when(ok(d) & (z > 0))(lambda: zhop(d, False).start())
+    def own_line(d):
+        def go():
+            if d < 0:
+                rc(out_ref.at[0], pc.block(pc.own, z + d), zs.at[0, -d - 1], zr.at[0, -d - 1], pc.dev(pc.own)).wait_recv()
+            if d > 0:
+                rc(out_ref.at[0], pc.block(pc.own, z + d), zs.at[1, d - 1], zr.at[1, d - 1], pc.dev(pc.own)).wait_recv()
+            if d <= 0:
+                pl.when(z < 3)(lambda: zhop(d, True).start())
+            if d >= 0:
+                pl.when(z > 0)(lambda: zhop(d, False).start())
+            hop(0, d, "f").start()
+            hop(0, d, "s").start()
+            hop(0, d, "b").start()
+        when(True if d == 0 else ok(d), go)
+    def first_col(d):
+        def go():
+            blk = pc.block(pc.cols[1], z + d)
+            rc(out_ref.at[0], blk, fs.at[d + 3], fr.at[d + 3], pc.dev(pc.own)).wait_recv()
+            hop(1, d, "s").start()
+            hop(1, d, "b").start()
+        when(True if d == 0 else ok(d), go)
+    def last_cols(d):
+        def go():
+            for col, j in ((2, 0), (3, 1)):
+                blk = pc.block(pc.cols[col], z + d)
+                rc(out_ref.at[0], blk, ss.at[j, d + 3], sr.at[j, d + 3], pc.dev(pc.own)).wait_recv()
+                hop(col, d, "b").start()
+        when(True if d == 0 else ok(d), go)
+    own_line(0)
+    for s in (1, 2, 3):
+        own_line(-s); own_line(s)
+        if s == 1:
+            first_col(0)
+        else:
+            first_col(-(s - 1)); first_col(s - 1)
+    first_col(-3); first_col(3)
+    for d in (0, -1, 1, -2, 2, -3, 3):
+        last_cols(d)
+    for d in (0, -1, 1, -2, 2, -3, 3):
+        def go():
+            for j in range(4):
+                blk = pc.block(pc.sib_cols[j], z + d)
+                rc(out_ref.at[0], blk, bs.at[j, d + 3], br.at[j, d + 3], pc.dev(pc.own)).wait_recv()
+            hop(0, d, "f").wait_send()
+            for col in (0, 1):
+                hop(col, d, "s").wait_send()
+            for col in range(4):
+                hop(col, d, "b").wait_send()
+            if d <= 0:
+                pl.when(z < 3)(lambda: zhop(d, True).wait_send())
+            if d >= 0:
+                pl.when(z > 0)(lambda: zhop(d, False).wait_send())
+        when(True if d == 0 else ok(d), go)
+    mine.wait()
+
+def gather_all(x, cid):
+    rows, width = x.shape
+    D = pltpu.SemaphoreType.DMA
+    out = pl.pallas_call(
+        gather_kernel,
+        out_shape=jax.ShapeDtypeStruct((32, rows, width), x.dtype),
+        in_specs=[pl.BlockSpec(memory_space=pltpu.VMEM)],
+        out_specs=pl.BlockSpec(memory_space=pl.ANY),
+        scratch_shapes=[D, D((2, 4)), D((2, 4)), D((7,)), D((7,)), D((2, 7)), D((2, 7)), D((4, 7)), D((4, 7))],
+        compiler_params=pltpu.CompilerParams(collective_id=cid, has_side_effects=True),
+        name="gather_all",
+    )(x)
+    return out.reshape(32 * rows, width)
+
+def scatter_kernel(p_ref, out_ref, acc, sib, sec, fst, zin, ld, bs, br, ss, sr, fs, fr, zs, zr):
+    pc = Place()
+    z = pc.z
+    rows = p_ref.shape[1]
+    inner = lax.rem(lax.div(z + 1, 2), 2)
+    low = 1 - lax.div(z, 2)
+    gray = (0, 1, 3, 2)
+    def group(k):
+        v = (1 - inner) * k + inner * gray[k]
+        return low * (3 - v) + (1 - low) * v
+    def rc(src, dst, s, r, dev):
+        return pltpu.make_async_remote_copy(src_ref=src, dst_ref=dst, send_sem=s, recv_sem=r, device_id=dev, device_id_type=MESH)
+    def load(k, col):
+        return pltpu.make_async_copy(p_ref.at[pc.block(pc.cols[col], group(k))], acc.at[k, col], ld.at[k, col])
+    def to_sib(k, col):
+        return rc(p_ref.at[pc.block(pc.sib_cols[col], group(k))], sib.at[k, col], bs.at[k, col], br.at[k, col], pc.dev(pc.sib))
+    def to_second(k, j):
+        return rc(acc.at[k, 2 + j], sec.at[k, j], ss.at[k, j], sr.at[k, j], pc.dev(pc.cols[2]))
+    def to_first(k):
+        return rc(acc.at[k, 1], fst.at[k], fs.at[k], fr.at[k], pc.dev(pc.cols[1]))
+    def to_z(k, up):
+        g = group(k)
+        i = 0 if up else 1
+        return rc(acc.at[k, 0], zin.at[i, g], zs.at[i, k], zr.at[i, g], pc.dev(pc.own, z + 1 if up else z - 1))
+    def from_z(g, i):
+        return rc(acc.at[0, 0], zin.at[i, g], zs.at[i, 0], zr.at[i, g], pc.dev(pc.own))
+    step = 16
+    def add(k, col, other):
+        def body(i, carry):
+            r = pl.ds(pl.multiple_of(i * step, step), step)
+            acc[k, col, r, :] = (acc[k, col, r, :].astype(jnp.float32) + other[r, :].astype(jnp.float32)).astype(acc.dtype)
+            return carry
+        lax.fori_loop(0, rows // step, body, 0)
+    for k in range(4):
+        for col in (2, 3, 1, 0):
+            load(k, col).start()
+    greet(pc, 4)
+    for k in range(4):
+        for col in (2, 3, 1, 0):
+            to_sib(k, col).start()
+    def join(k, col):
+        load(k, col).wait()
+        to_sib(k, col).wait_recv()
+        add(k, col, sib.at[k, col])
+    def stage_a(k):
+        for j in (0, 1):
+            join(k, 2 + j)
+            to_second(k, j).start()
+    def stage_b(k):
+        join(k, 1)
+        to_second(k, 1).wait_recv()
+        add(k, 1, sec.at[k, 1])
+        to_first(k).start()
+        join(k, 0)
+    def stage_c(k):
+        to_second(k, 0).wait_recv()
+        add(k, 0, sec.at[k, 0])
+        to_first(k).wait_recv()
+        add(k, 0, fst.at[k])
+        g = group(k)
+        if k < 3:
+            @pl.when(g > z)
+            def _():
+                @pl.when(z > 0)
+                def _():
+                    from_z(g, 0).wait_recv()
+                    add(k, 0, zin.at[0, g])
+                to_z(k, True).start()
+            @pl.when(g < z)
+            def _():
+                @pl.when(z < 3)
+                def _():
+                    from_z(g, 1).wait_recv()
+                    add(k, 0, zin.at[1, g])
+                to_z(k, False).start()
+        else:
+            @pl.when(z > 0)
+            def _():
+                from_z(z, 0).wait_recv()
+                add(k, 0, zin.at[0, z])
+            @pl.when(z < 3)
+            def _():
+                from_z(z, 1).wait_recv()
+                add(k, 0, zin.at[1, z])
+    stage_a(0); stage_a(1); stage_b(0); stage_a(2); stage_b(1); stage_c(0)
+    stage_a(3); stage_b(2); stage_c(1); stage_b(3); stage_c(2); stage_c(3)
+    out_ref[...] = acc[3, 0]
+    for k in range(4):
+        for col in range(4):
+            to_sib(k, col).wait_send()
+        for j in (0, 1):
+            to_second(k, j).wait_send()
+        to_first(k).wait_send()
+        if k < 3:
+            pl.when(group(k) > z)(lambda: to_z(k, True).wait_send())
+            pl.when(group(k) < z)(lambda: to_z(k, False).wait_send())
+
+def scatter_all(p, cid):
+    total, width = p.shape
+    rows = total // 32
+    D = pltpu.SemaphoreType.DMA
+    V = lambda *s: pltpu.VMEM(s + (rows, width), p.dtype)
+    return pl.pallas_call(
+        scatter_kernel,
+        out_shape=jax.ShapeDtypeStruct((rows, width), p.dtype),
+        in_specs=[pl.BlockSpec(memory_space=pl.ANY)],
+        out_specs=pl.BlockSpec(memory_space=pltpu.VMEM),
+        scratch_shapes=[V(4, 4), V(4, 4), V(4, 2), V(4), V(2, 4), D((4, 4)), D((4, 4)), D((4, 4)), D((4, 2)), D((4, 2)), D((4,)), D((4,)), D((2, 4)), D((2, 4))],
+        compiler_params=pltpu.CompilerParams(collective_id=cid, has_side_effects=True, vmem_limit_bytes=48 << 20),
+        name="scatter_all",
+    )(p.reshape(32, rows, width))
+
+
+def attend_kernel(qkv_ref, att_ref, lse_ref):
+    length = qkv_ref.shape[0]
+    tile = 256
+    heads = att_ref.shape[1] // HEAD_DIM
+    for head in range(heads):
+        at = lambda part: pl.ds((part * heads + head) * HEAD_DIM, HEAD_DIM)
+        for first in range(0, length, tile):
+            last = first + tile
+            q = qkv_ref[pl.ds(first, tile), at(0)]
+            k = qkv_ref[pl.ds(0, last), at(1)]
+            v = qkv_ref[pl.ds(0, last), at(2)]
+            scores = lax.dot_general(
+                k, q, (((1,), (1,)), ((), ())), preferred_element_type=jnp.float32
+            ) * HEAD_DIM ** (-0.5)
+            key_pos = lax.broadcasted_iota(jnp.int32, scores.shape, 0)
+            query_pos = first + lax.broadcasted_iota(jnp.int32, scores.shape, 1)
+            scores = jnp.where(key_pos <= query_pos, scores, -1e30)
+            highest = jnp.max(scores, axis=0, keepdims=True)
+            exponent = jnp.exp(scores - highest)
+            total = jnp.sum(exponent, axis=0, keepdims=True)
+            mixed = lax.dot_general(
+                v,
+                exponent.astype(jnp.bfloat16),
+                (((0,), (0,)), ((), ())),
+                preferred_element_type=jnp.float32,
+            )
+            mixed = mixed * (1.0 / total)
+            att_ref[pl.ds(first, tile), pl.ds(head * HEAD_DIM, HEAD_DIM)] = mixed.T.astype(
+                jnp.bfloat16
+            )
+            lse_ref[0, pl.ds(head, 1), pl.ds(first, tile)] = highest + jnp.log(total)
+
+
+def attend(qkv, slots):
+    rows, width = qkv.shape
+    length = rows // slots
+    out = width // 3
+    return pl.pallas_call(
+        attend_kernel,
+        grid=(slots,),
+        out_shape=(
+            jax.ShapeDtypeStruct((rows, out), jnp.bfloat16),
+            jax.ShapeDtypeStruct((slots, out // HEAD_DIM, length), jnp.float32),
+        ),
+        in_specs=[pl.BlockSpec((length, width), lambda s: (s, 0))],
+        out_specs=(
+            pl.BlockSpec((length, out), lambda s: (s, 0)),
+            pl.BlockSpec((1, out // HEAD_DIM, length), lambda s: (s, 0, 0)),
+        ),
+        compiler_params=pltpu.CompilerParams(vmem_limit_bytes=48 << 20),
+        name="attend",
+    )(qkv)
+
+
+def attend_back_kernel(qkv_ref, du_ref, lse_ref, gate_ref, dqkv_ref, dgate_ref, dk_acc, dv_acc):
+    length = qkv_ref.shape[0]
+    tile = 256
+    heads = du_ref.shape[1] // HEAD_DIM
+    scale = HEAD_DIM ** (-0.5)
+    for head in range(heads):
+        at = lambda part: pl.ds((part * heads + head) * HEAD_DIM, HEAD_DIM)
+        dk_acc[...] = jnp.zeros_like(dk_acc)
+        dv_acc[...] = jnp.zeros_like(dv_acc)
+        for first in range(0, length, tile):
+            last = first + tile
+            q = qkv_ref[pl.ds(first, tile), at(0)]
+            k = qkv_ref[pl.ds(0, last), at(1)]
+            v = qkv_ref[pl.ds(0, last), at(2)]
+            du = du_ref[pl.ds(first, tile), pl.ds(head * HEAD_DIM, HEAD_DIM)]
+            gate = gate_ref[0, :, pl.ds(first, tile)]
+            lse = lse_ref[0, pl.ds(head, 1), pl.ds(first, tile)]
+            scores = (
+                lax.dot_general(k, q, (((1,), (1,)), ((), ())), preferred_element_type=jnp.float32)
+                * scale
+            )
+            key_pos = lax.broadcasted_iota(jnp.int32, scores.shape, 0)
+            query_pos = first + lax.broadcasted_iota(jnp.int32, scores.shape, 1)
+            probs = jnp.where(key_pos <= query_pos, jnp.exp(scores - lse), 0.0)
+            d_prob = lax.dot_general(
+                v, du, (((1,), (1,)), ((), ())), preferred_element_type=jnp.float32
+            )
+            along = jnp.sum(probs * d_prob, axis=0, keepdims=True)
+            dgate_ref[0, pl.ds(head, 1), pl.ds(first, tile)] = along
+            shared = probs * gate
+            d_scores = (shared * (d_prob - along)).astype(jnp.bfloat16)
+            dq = lax.dot_general(
+                d_scores, k, (((0,), (0,)), ((), ())), preferred_element_type=jnp.float32
+            )
+            dqkv_ref[pl.ds(first, tile), at(0)] = (dq * scale).astype(jnp.bfloat16)
+            dk_acc[pl.ds(0, last), :] += jnp.dot(d_scores, q, preferred_element_type=jnp.float32)
+            dv_acc[pl.ds(0, last), :] += jnp.dot(
+                shared.astype(jnp.bfloat16), du, preferred_element_type=jnp.float32
+            )
+        dqkv_ref[:, at(1)] = (dk_acc[...] * scale).astype(jnp.bfloat16)
+        dqkv_ref[:, at(2)] = dv_acc[...].astype(jnp.bfloat16)
+
+
+def attend_back(qkv, du, lse, gate, slots):
+    rows, width = qkv.shape
+    length = rows // slots
+    out = width // 3
+    heads = out // HEAD_DIM
+    return pl.pallas_call(
+        attend_back_kernel,
+        grid=(slots,),
+        out_shape=(
+            jax.ShapeDtypeStruct((rows, width), jnp.bfloat16),
+            jax.ShapeDtypeStruct((slots, heads, length), jnp.float32),
+        ),
+        in_specs=[
+            pl.BlockSpec((length, width), lambda s: (s, 0)),
+            pl.BlockSpec((length, out), lambda s: (s, 0)),
+            pl.BlockSpec((1, heads, length), lambda s: (s, 0, 0)),
+            pl.BlockSpec((1, 1, length), lambda s: (s, 0, 0)),
+        ],
+        out_specs=(
+            pl.BlockSpec((length, width), lambda s: (s, 0)),
+            pl.BlockSpec((1, heads, length), lambda s: (s, 0, 0)),
+        ),
+        scratch_shapes=[
+            pltpu.VMEM((length, HEAD_DIM), jnp.float32),
+            pltpu.VMEM((length, HEAD_DIM), jnp.float32),
+        ],
+        compiler_params=pltpu.CompilerParams(vmem_limit_bytes=48 << 20),
+        name="attend_back",
+    )(qkv, du, lse, gate)
+
+
+def spread(per_token):
+    columns = per_token.T.reshape(1, -1)
+    whole = lax.all_gather(columns, EVERY, axis=0, tiled=True)
+    return whole.reshape(whole.shape[0], per_token.shape[1], per_token.shape[0])
+
+
+def home_sums(per_expert, experts):
+    devices, tokens = per_expert.shape
+    mine = (jnp.arange(experts) == lax.axis_index("expert")).astype(jnp.float32)
+    columns = (per_expert[:, None, :] * mine[None, :, None]).reshape(devices, experts * tokens)
+    return lax.psum_scatter(columns, EVERY, scatter_dimension=0, tiled=True).reshape(experts, tokens).T
+
+
+def placed_weights(
+    layer_input,
+    output_grad,
+    lengths,
+    attn_routes,
+    ffn_routes,
+    norm1_gain,
+    norm2_gain,
+    attn_router,
+    ffn_router,
+    w_kv,
+    w_query,
+    w_out,
+    w_in,
+    w_down,
+):
+    f32, low = jnp.float32, jnp.bfloat16
+    tokens, width = layer_input.shape[1:]
+    experts = lax.axis_size("expert")
+    contexts = lax.axis_size("context")
+    slots = lax.axis_size("dp")
+    shares = contexts * slots
+    devices = experts * shares
+    own_expert = lax.axis_index("expert")
+    capacity = tokens * TOP // experts + tokens // 32
+    room = -(-capacity // 8) * 8
+
+    position = lax.axis_index(("expert", "context")) * tokens + jnp.arange(tokens, dtype=jnp.int32)
+    live = (position < lengths[0]).astype(f32)
+    x_float = layer_input[0].astype(f32)
+    scale_one = rms_scale(x_float)
+    normed_one = (x_float * scale_one * norm1_gain).astype(low)
+    grad_out = output_grad[0].astype(f32) * live[:, None]
+
+    kv_parts = w_kv.reshape(-1, 2, shares, QD // shares).transpose(0, 2, 1, 3)
+    qkv_parts = jnp.concatenate(
+        [w_query[0].reshape(-1, shares, QD // shares), kv_parts.reshape(kv_parts.shape[0], shares, -1)],
+        axis=2,
+    )
+    piece = qkv_parts.shape[2]
+    w_qkv = lax.all_to_all(
+        qkv_parts.reshape(-1, shares * piece), SHARE, split_axis=1, concat_axis=0, tiled=True
+    )
+    w_pair = lax.all_to_all(w_in[0], "context", split_axis=0, concat_axis=0, tiled=True)
+    moves = [(s, (s % contexts) * slots + s // contexts) for s in range(shares)]
+    w_unit = lax.ppermute(w_down[0], SHARE, moves)
+    units = w_unit.shape[0]
+
+    all_one = gather_all(normed_one, 0)
+    shares_a, picked_a = pair_gates(
+        jnp.dot(normed_one, attn_router, preferred_element_type=f32), attn_routes[0], live, experts
+    )
+    gates_a = jnp.sum(shares_a[:, :, None] * picked_a, axis=1)
+    named_f = jnp.sum(
+        (ffn_routes[0][:, :, None] == jnp.arange(experts, dtype=jnp.int32)).astype(f32), axis=1
+    )
+    aux = lax.dynamic_index_in_dim(
+        spread(jnp.concatenate([gates_a, named_f * live[:, None]], axis=1)).reshape(
+            devices, 2, experts, tokens
+        ),
+        own_expert,
+        axis=2,
+        keepdims=False,
+    )
+    gate_a, named = aux[:, 0], aux[:, 1]
+    all_grad = lax.all_gather(grad_out.astype(low), EVERY, axis=0, tiled=True)
+    qkv = jnp.dot(all_one, w_qkv, preferred_element_type=f32).astype(low)
+    attended, lse = attend(qkv, slots)
+    gated = (attended.astype(f32) * gate_a.reshape(-1, 1)).astype(low)
+    h1_part = jnp.dot(gated, w_out[0], preferred_element_type=f32).astype(low)
+    residual_one = x_float + scatter_all(h1_part, 1).astype(f32)
+
+    scale_two = rms_scale(residual_one)
+    normed_two = (residual_one * scale_two * norm2_gain).astype(low)
+    all_two = gather_all(normed_two, 2)
+    shares_f, picked_f = pair_gates(
+        jnp.dot(normed_two, ffn_router, preferred_element_type=f32), ffn_routes[0], live, experts
+    )
+    gates_f = jnp.sum(shares_f[:, :, None] * picked_f, axis=1)
+    gate_f = lax.dynamic_index_in_dim(spread(gates_f), own_expert, axis=1, keepdims=False)
+    earlier = (jnp.arange(tokens)[:, None] < jnp.arange(tokens)[None, :]).astype(f32)
+    rank = jnp.dot(named, earlier, preferred_element_type=f32)
+    table = jnp.where(
+        rank[:, None, :] == jnp.arange(room, dtype=f32)[None, :, None], named[:, None, :], 0.0
+    )
+    low_table = table.astype(low)
+
+    def pick(whole):
+        rows = jnp.einsum(
+            "bst,btd->bsd",
+            low_table,
+            whole.reshape(devices, tokens, width),
+            preferred_element_type=f32,
+        )
+        return rows.astype(low).reshape(devices * room, width)
+
+    def put(rows):
+        whole = jnp.einsum(
+            "bst,bsd->btd", low_table, rows.reshape(devices, room, width), preferred_element_type=f32
+        )
+        return whole.astype(low).reshape(devices * tokens, width)
+
+    row_gate = jnp.sum(table * gate_f[:, None, :], axis=2).reshape(-1, 1)
+    routed = pick(all_two)
+    both = lax.dot_general(routed, w_pair, (((1,), (1,)), ((), ())), preferred_element_type=f32)
+    gate_part, up_part = both[:, :units], both[:, units:]
+    sigmoid_gate = jax.nn.sigmoid(gate_part)
+    hidden_f = gate_part * sigmoid_gate * up_part
+    hidden = hidden_f.astype(low)
+    down = (jnp.dot(hidden, w_unit, preferred_element_type=f32) * row_gate).astype(low)
+    mixed = scatter_all(put(down), 3).astype(f32)
+    layer_output = (live[:, None] * (residual_one + mixed)).astype(low)
+
+    d_rows = pick(all_grad)
+    d_plain = lax.dot_general(d_rows, w_unit, (((1,), (1,)), ((), ())), preferred_element_type=f32)
+    row_sums = jnp.sum(d_plain * hidden.astype(f32), axis=1).reshape(devices, room)
+    dgate_f = home_sums(jnp.sum(table * row_sums[:, :, None], axis=1), experts)
+    d_hidden = d_plain * row_gate
+    d_gate = d_hidden * up_part * sigmoid_gate * (1.0 + gate_part * (1.0 - sigmoid_gate))
+    d_up = d_hidden * gate_part * sigmoid_gate
+    d_both = jnp.concatenate([d_gate, d_up], axis=1).astype(low)
+    d_two_part = put(jnp.dot(d_both, w_pair, preferred_element_type=f32).astype(low))
+    grad_unit = lax.dot_general(
+        (hidden.astype(f32) * row_gate).astype(low),
+        d_rows,
+        (((0,), (0,)), ((), ())),
+        preferred_element_type=f32,
+    )
+    grad_pair = lax.dot_general(
+        d_both, routed, (((0,), (0,)), ((), ())), preferred_element_type=f32
+    )
+    grad_w_in = lax.all_to_all(
+        grad_pair.astype(low), "context", split_axis=0, concat_axis=0, tiled=True
+    ).astype(f32)
+    grad_w_down = lax.ppermute(grad_unit.astype(low), SHARE, [(b, a) for a, b in moves]).astype(f32)
+    dlog_f = gates_f * (dgate_f - jnp.sum(gates_f * dgate_f, axis=1, keepdims=True))
+    d_normed_two = scatter_all(d_two_part, 4).astype(f32) + jnp.dot(
+        dlog_f, ffn_router.astype(f32).T, precision=PRECISE
+    )
+    local_ffn_router = jnp.dot(normed_two.astype(f32).T, dlog_f, precision=PRECISE)
+    d_mid, local_gain_two = norm_back(residual_one, scale_two, norm2_gain, d_normed_two)
+    d_residual = grad_out + d_mid
+
+    all_mid = gather_all(d_residual.astype(low), 5)
+    d_att = lax.dot_general(
+        all_mid, w_out[0], (((1,), (1,)), ((), ())), preferred_element_type=f32
+    ).astype(low)
+    d_qkv, head_sums = attend_back(
+        qkv, d_att, lse, gate_a.reshape(slots, 1, -1), slots
+    )
+    grad_w_out = lax.dot_general(
+        gated, all_mid, (((0,), (0,)), ((), ())), preferred_element_type=f32
+    )
+    dgate_a = home_sums(jnp.sum(head_sums, axis=1).reshape(devices, tokens), experts)
+    d_one_part = lax.dot_general(
+        d_qkv, w_qkv, (((1,), (1,)), ((), ())), preferred_element_type=f32
+    ).astype(low)
+    grad_qkv = lax.dot_general(
+        all_one, d_qkv, (((0,), (0,)), ((), ())), preferred_element_type=f32
+    ).astype(low)
+    grad_parts = lax.all_to_all(grad_qkv, SHARE, split_axis=0, concat_axis=1, tiled=True)
+    grad_parts = grad_parts.reshape(-1, shares, piece)
+    grad_w_query = grad_parts[:, :, : QD // shares].reshape(-1, QD).astype(f32)
+    kv_grads = grad_parts[:, :, QD // shares :].reshape(-1, shares, 2, QD // shares)
+    grad_w_kv = lax.psum(kv_grads.transpose(0, 2, 1, 3).reshape(-1, 2 * QD), "expert").astype(f32)
+    dlog_a = gates_a * (dgate_a - jnp.sum(gates_a * dgate_a, axis=1, keepdims=True))
+    d_normed_one = scatter_all(d_one_part, 6).astype(f32) + jnp.dot(
+        dlog_a, attn_router.astype(f32).T, precision=PRECISE
+    )
+    local_attn_router = jnp.dot(normed_one.astype(f32).T, dlog_a, precision=PRECISE)
+    d_first, local_gain_one = norm_back(x_float, scale_one, norm1_gain, d_normed_one)
+    input_grad = d_residual + d_first
+    gain_one_sum, gain_two_sum, router_a_sum, router_f_sum = lax.psum(
+        (local_gain_one, local_gain_two, local_attn_router, local_ffn_router),
+        ("expert", "context", "dp"),
+    )
+    return (
+        layer_output[None],
+        input_grad[None],
+        gain_one_sum,
+        gain_two_sum,
+        router_a_sum,
+        router_f_sum,
+        grad_w_kv,
+        grad_w_query[None],
+        grad_w_out[None],
+        grad_w_in[None],
+        grad_w_down[None],
+    )
+
+
+def fits_in_place(mesh):
+    sizes = (mesh.shape["expert"], mesh.shape["context"], mesh.shape["dp"])
+    return sizes == (4, 2, 4)
+
+
 def solution(mesh):
     placed = (
         P("dp", ("expert", "context"), None),
@@ -431,7 +1023,7 @@
         P("expert", ("context", "dp"), None),
     )
     return jax.shard_map(
-        on_device,
+        placed_weights if fits_in_place(mesh) else gathered_weights,
         mesh=mesh,
         in_specs=placed,
         out_specs=(

time: 4080 us -> 1570 us (0.38)
  waiting for transfers between devices: 3410 us -> 167 us
  Pallas kernels: 0 us -> 918 us
  matrix products: 367 us -> 235 us
  local copies, waits for them, and re-layouts: 113 us -> 34.2 us
    all_gather x8 -> x1, waiting for transfers between devices: 1630 us -> 0.02 us  [placed_weights(): all_grad = lax.all_gather(grad_out.astype(low), EVERY, axis=0, tiled=True)]
    pallas_call x0 -> x9, Pallas kernels: none -> 918 us  [the longest x3 494 us: gather_all(): pl.pallas_call(gather_kernel, out_shape=jax.ShapeDtypeStruct((32, rows, w...]
    reduce_scatter x4 -> x0, waiting for transfers between devices: 788 us -> none  [weight_grad(): lax.psum_scatter(lax.dot_general(left_rows, gradient, (((0,), (0,)), ((),...]
    unnamed x16 -> x7, waiting for transfers between devices: 727 us -> 0.1 us
    dot_general x62 -> x23, matrix products: 367 us -> 235 us  [the longest x2 24.1 us: pick(): jnp.einsum('bst,btd->bsd', low_table, whole.reshape(devices, tokens, widt...]
    all_gather x2, blocking collectives: 33.3 us -> 112 us  [spread(): whole = lax.all_gather(columns, EVERY, axis=0, tiled=True)]
    all_to_all x8 -> x4, waiting for transfers between devices: 86.1 us -> 27.3 us  [the longest x1 27.3 us: placed_weights(): lax.all_to_all(grad_qkv, SHARE, split_axis=0, concat_axis=1, tiled=True)]
  transfers between devices with their start and end apart: 23 -> 11, of which waited for: 21 -> 3; matrix products, arithmetic and copies ran while one was open for 10% -> 17% of each run, Pallas kernels for 0% -> 59%
where the time goes in v1:
time: 1570 us; the launch traced here: 1560 us
  Pallas kernels  918 us (58%)
  matrix products  235 us (15%)
  waiting for transfers between devices  167 us (11%)
  blocking collectives  112 us (7%)
  other arithmetic  47.4 us (3%)
  local copies, waits for them, and re-layouts  34.2 us (2%)
  starting transfers between devices  32.4 us (2%)
    pallas_call x3, Pallas kernels, gather_all(): pl.pallas_call(gather_kernel, out_shape=jax.ShapeDtypeStruct((32, rows, w...  494 us
    pallas_call x4, Pallas kernels, scatter_all(): pl.pallas_call(scatter_kernel, out_shape=jax.ShapeDtypeStruct((rows, widt...  385 us
    psum x1, waiting for transfers between devices, placed_weights(): lax.psum((local_gain_one, local_gain_two, local_attn_router, local_ffn_ro...  128 us
    all_gather x2, blocking collectives, spread(): whole = lax.all_gather(columns, EVERY, axis=0, tiled=True)  112 us
  transfers between devices with their start and end apart: 11, of which 3 were waited for; matrix products, arithmetic and copies ran while one was open for 17% of the time, Pallas kernels for 59%

profile of v1, /device:TPU:8, one launch (start us, length us, event | category | flops | bytes accessed | tf_op | source)
XLA Modules:
  0.0 1562.9 jit_solution(13647945866980614481)
XLA Ops:
  8.0 2.0 fusion.17
  10.0 2.2 copy.64
  12.2 1.6 copy.72
  13.9 2.6 reshape.290
  16.5 1.5 copy.58
  18.5 3.5 pad_maximum_fusion.3
  22.0 6.2 all-to-all-start
  28.3 3.4 collective-permute-start
  33.9 322.4 %gather_all.3 = bf16[32,128,2048]{2,1,0:T(8,128)(2,1)} custom-call(bf16[128,2048]{1,0:T(8,128)(2,1)} %fusion.8.x_ref), custom_call_target="tpu_custom_call" | custom-call | tf_op jit(solution)/shard_map/gather_all/pallas_call | solution.py:547
  357.3 60.2 %all-gather = f32[32,1,1024]{2,1,0:T(1,128)S(1)} all-gather(f32[1,1,1024]{2,1,0:T(1,128)S(1)} %bitcast.173), channel_id=1, replica_groups=mesh['expert'=4,'context'=2,'dp'=4] {'dp','expert','context'}, dimensions={0}, use_global_device_ids=true | all-gather | bytes 135168 | tf_op jit(solution)/shard_map/all_gather | solution.py:801
  419.0 6.2 all-to-all-start.1
  425.8 19.4 %convolution_convert_fusion.6.qkv_ref = bf16[4096,768]{1,0:T(8,128)(2,1)} fusion(bf16[4096,2048]{1,0:T(8,128)(2,1)} %bitcast.147, bf16[2048,768]{1,0:T(8,128)(2,1)} %bitcast.7), kind=kOutput, calls=%fused_computation.9 | convolution fusion | flops 12888047616 | bytes 26214400 | tf_op jit(solution)/shard_map/dot_general | solution.py:878
  445.2 15.1 attend.1
  460.3 8.1 convolution_convert_fusion.1
  468.4 85.4 %scatter_all.4 = bf16[128,2048]{1,0:T(8,128)(2,1)S(1)} custom-call(bf16[32,128,2048]{2,1,0:T(8,128)(2,1)} %bitcast.139), custom_call_target="tpu_custom_call" | custom-call | tf_op jit(solution)/shard_map/scatter_all/pallas_call | solution.py:660
  555.7 96.7 %gather_all.4 = bf16[32,128,2048]{2,1,0:T(8,128)(2,1)} custom-call(bf16[128,2048]{1,0:T(8,128)(2,1)} %multiply_convert_fusion.6.x_ref), custom_call_target="tpu_custom_call" | custom-call | tf_op jit(solution)/shard_map/gather_all/pallas_call | solution.py:547
  652.4 12.1 convolution_convert_fusion.8
  664.6 19.7 %fusion.48 = f32[2304,1408]{0,1:T(8,128)} fusion(bf16[2304,2048]{1,0:T(8,128)(2,1)} %bitcast.141, bf16[1408,2048]{1,0:T(8,128)(2,1)} %bitcast.20), kind=kOutput, calls=%fused_computation.127 | convolution fusion | flops 13287555072 | bytes 28180480 | tf_op jit(solution)/shard_map/dot_general | solution.py:916
  684.7 52.3 %all-gather.1 = f32[32,1,512]{2,1,0:T(1,128)S(1)} all-gather(f32[1,1,512]{2,1,0:T(1,128)S(1)} %bitcast.166), channel_id=1, replica_groups=mesh['expert'=4,'context'=2,'dp'=4] {'dp','expert','context'}, dimensions={0}, use_global_device_ids=true | all-gather | bytes 67584 | tf_op jit(solution)/shard_map/all_gather | solution.py:801
  737.0 12.0 convolution_convert_fusion.7
  749.0 16.6 %fusion = (f32[2304]{0:T(1024)S(1)}, bf16[2304,704]{0,1:T(8,128)(2,1)}, f32[2304,704]{0,1:T(8,128)}) fusion(f32[2304,1408]{0,1:T(8,128)} %fusion.48, bf16[2304,2048]{1,0:T(8,128)(2,1)} %bitcast.143, bf16[704,2048]{1,0:T(8,128)(2,1)} %collective-permute-done), kind=kOutput, calls=%fused_computation.10 | convolution fusion | flops 6658373632 | bytes 35038208 | tf_op jit(solution)/shard_map/dot_general | solution.py:926
  765.7 1.1 fusion.5
  766.9 10.6 multiply_convert_fusion.2
  779.4 8.1 convolution_convert_fusion.11
  787.5 2.4 collective-permute-start.1
  789.9 11.6 multiply_convert_fusion
  801.5 10.5 convolution_convert_fusion.3.p_ref
  812.6 20.4 %convolution_convert_fusion.4 = bf16[2304,2048]{1,0:T(8,128)(2,1)} fusion(bf16[1408,2048]{1,0:T(8,128)(2,1)} %bitcast.20, bf16[2304,704]{0,1:T(8,128)(2,1)} %get-tuple-element.34, bf16[2304,704]{0,1:T(8,128)(2,1)} %get-tuple-element.33), kind=kOutput, calls=%fused_computation.5 | convolution fusion | flops 13305249792 | bytes 21692416 | tf_op jit(solution)/shard_map/dot_general | solution.py:933
  833.0 10.6 convolution_convert_fusion.2.p_ref
  843.5 118.4 %scatter_all.5 = bf16[128,2048]{1,0:T(8,128)(2,1)S(1)} custom-call(bf16[32,128,2048]{2,1,0:T(8,128)(2,1)} %convolution_convert_fusion.3.p_ref), custom_call_target="tpu_custom_call" | custom-call | tf_op jit(solution)/shard_map/scatter_all/pallas_call | solution.py:660
  962.0 83.0 %scatter_all.6 = bf16[128,2048]{1,0:T(8,128)(2,1)S(1)} custom-call(bf16[32,128,2048]{2,1,0:T(8,128)(2,1)} %convolution_convert_fusion.2.p_ref), custom_call_target="tpu_custom_call" | custom-call | tf_op jit(solution)/shard_map/scatter_all/pallas_call | solution.py:660
  1045.0 1.3 constant_dynamic-slice_fusion.1
  1046.4 1.5 multiply_reduce_fusion
  1048.0 3.0 fusion.44
  1051.0 74.9 %gather_all.5 = bf16[32,128,2048]{2,1,0:T(8,128)(2,1)} custom-call(bf16[128,2048]{1,0:T(8,128)(2,1)} %get-tuple-element.29.x_ref), custom_call_target="tpu_custom_call" | custom-call | tf_op jit(solution)/shard_map/gather_all/pallas_call | solution.py:547
  1125.9 8.4 convolution_convert_fusion.9.du_ref
  1134.2 24.5 %attend_back.1 = (bf16[4096,768]{1,0:T(8,128)(2,1)}, f32[4,2,1024]{2,1,0:T(2,128)S(1)}) custom-call(bf16[4096,768]{1,0:T(8,128)(2,1)} %convolution_convert_fusion.6.qkv_ref, bf16[4096,256]{1,0:T(8,128)(2,1)S(1)} %convolution_convert_fusion.9.du_ref, f32[4,2,1024]{2,1,0:T(2,128)S(1)} %get-tuple-element.16.lse_ref, f32[4,1,1024]{2,1,0:T(1,128)S(1)} %bitcast.136), custom_call_target="tpu_custom_call" | custom-call | tf_op jit(solution)/shard_map/attend_back/pallas_call | solution.py:773
  1158.8 20.3 %convolution_convert_fusion.10 = bf16[2048,768]{1,0:T(8,128)(2,1)} fusion(bf16[4096,2048]{1,0:T(8,128)(2,1)} %bitcast.148, bf16[4096,768]{1,0:T(8,128)(2,1)} %get-tuple-element.17), kind=kOutput, calls=%fused_computation.22 | convolution fusion | flops 12886474752 | bytes 26214400 | tf_op jit(solution)/shard_map/dot_general | solution.py:969
  1179.1 7.5 all-to-all-start.2
  1186.6 20.3 %convolution_convert_fusion.5 = bf16[1408,2048]{1,0:T(8,128)(2,1)} fusion(bf16[2304,2048]{1,0:T(8,128)(2,1)} %bitcast.142, bf16[2304,704]{0,1:T(8,128)(2,1)} %get-tuple-element.34, bf16[2304,704]{0,1:T(8,128)(2,1)} %get-tuple-element.33), kind=kOutput, calls=%fused_computation.8 | convolution fusion | flops 13303414784 | bytes 21692416 | tf_op jit(solution)/shard_map/dot_general | solution.py:940
  1207.6 20.1 %convolution_convert_fusion = bf16[4096,2048]{1,0:T(8,128)(2,1)} fusion(bf16[4096,768]{1,0:T(8,128)(2,1)} %get-tuple-element.17, bf16[2048,768]{1,0:T(8,128)(2,1)} %bitcast.7), kind=kOutput, calls=%fused_computation.1 | convolution fusion | flops 12893290496 | bytes 26214400 | tf_op jit(solution)/shard_map/dot_general | solution.py:966
  1227.7 27.3 %all-to-all-done.2 = bf16[8,256,768]{2,1,0:T(8,128)(2,1)} async-done(((bf16[8,256,768]{2,1,0:T(8,128)(2,1)}), bf16[8,256,768]{2,1,0:T(8,128)(2,1)}, u32[]{:S(2)}, u32[]{:S(2)}) %all-to-all-start.2) | async-done | bytes 3145760 | tf_op jit(solution)/shard_map/all_to_all | solution.py:972
  1254.9 6.1 all-to-all-start.3
  1261.1 1.8 slice.28
  1262.9 2.2 reshape.304
  1265.1 4.0 copy.62
  1269.1 2.2 copy.67
  1271.5 11.7 convolution_bitcast_fusion
  1283.3 97.8 %scatter_all.7 = bf16[128,2048]{1,0:T(8,128)(2,1)S(1)} custom-call(bf16[32,128,2048]{2,1,0:T(8,128)(2,1)} %bitcast.149), custom_call_target="tpu_custom_call" | custom-call | tf_op jit(solution)/shard_map/scatter_all/pallas_call | solution.py:660
  1382.0 1.3 constant_dynamic-slice_fusion
  1384.3 1.5 fusion.15
  1385.9 2.7 fusion.12
  1388.5 8.7 bitcast_convert_fusion
  1397.2 5.3 bitcast_convert_fusion.1
  1402.5 1.4 slice_convert_fusion
  1403.9 1.2 copy.63
  1405.2 1.5 reshape.308
  1406.7 12.0 all-reduce.8.cloned.1.call-done
  1418.6 4.1 convert_element_type.185
  1422.7 128.1 %all-reduce.14.cloned.1.call-done = (f32[2048]{0:T(1024)}, f32[2048]{0:T(1024)}, f32[2048,4]{0,1:T(4,128)}, f32[2048,4]{0,1:T(4,128)}) async-done(((f32[2048]{0:T(1024)}, f32[2048]{0:T(1024)}, f32[2048,4]{0,1:T(4,128)}, f32[2048,4]{0,1:T(4,128)}), (f32[2048]{0:T(1024)}, f32[2048]{0:T(1024)}, f32[2048,4]{0,1:T(4,128)}, f32[2048,4]{0,1:T(4,128)})) %all-reduce.14.cloned.1.call-update) | async-done | bytes 81936 | tf_op jit(solution)/shard_map/psum | solution.py:984
  1550.8 1.3 copy.82
  1552.1 1.3 copy.83
  1553.4 1.4 copy.84
  1554.8 1.4 copy.85
  (135 shorter events, 13.6 us)
Async XLA Ops:
  7.2 453.1 %copy-start = (bf16[1,256,2048]{2,1,0:T(8,128)(2,1)S(1)}, bf16[1,256,2048]{2,1,0:T(8,128)(2,1)}, u32[]{:S(2)}) copy-start(bf16[1,256,2048]{2,1,0:T(8,128)(2,1)} %param.25) | copy-start | bytes 3145732
  7.2 729.8 %all-gather.4.cloned.1.call-start = ((), (), s32[]{:S(2)}) async-start(), calls=%async_computation.4 | async-start | bytes 17301504 | tf_op jit(solution)/shard_map/all_gather | solution.py:877
  18.5 13.2 copy-start.6
  18.5 14.4 copy-start.18
  22.0 397.0 %all-to-all-start = ((bf16[256,8,768]{2,0,1:T(8,128)(2,1)}), bf16[256,8,768]{2,0,1:T(8,128)(2,1)}, u32[]{:S(2)}, u32[]{:S(2)}) async-start(bf16[256,8,768]{2,0,1:T(8,128)(2,1)} %pad_maximum_fusion.3), calls=%async_computation | async-start | bytes 6291456 | tf_op jit(solution)/shard_map/all_to_all | solution.py:852
  28.3 720.7 %collective-permute-start = (bf16[704,2048]{1,0:T(8,128)(2,1)}, bf16[704,2048]{1,0:T(8,128)(2,1)}, u32[]{:S(2)}, u32[]{:S(2)}) collective-permute-start(bf16[704,2048]{1,0:T(8,128)(2,1)} %bitcast.179), channel_id=1, source_target_pairs={{0,0},{1,4},{2,1},{3,5},{4,2},{5,6},{6,3},{7,7},{8,8},{9,12},{10,9... | collective-permute-start | bytes 8650760 | tf_op jit(solution)/shard_map/ppermute | solution.py:857
  32.4 0.6 copy-start.28
  33.9 322.5 %copy-start.10 = (bf16[128,2048]{1,0:T(8,128)(2,1)S(1)}, bf16[128,2048]{1,0:T(8,128)(2,1)}, u32[]{:S(2)}) copy-start(bf16[128,2048]{1,0:T(8,128)(2,1)} %fusion.8.x_ref) | copy-start | bytes 1572868
  33.9 322.5 %copy-start.24 = (bf16[2048,4]{0,1:T(4,128)(2,1)S(1)}, bf16[2048,4]{0,1:T(4,128)(2,1)}, u32[]{:S(2)}) copy-start(bf16[2048,4]{0,1:T(4,128)(2,1)} %param.21) | copy-start | bytes 49156
  33.9 322.7 %copy-start.27 = (s32[1,128,2]{1,2,0:T(2,128)S(1)}, s32[1,128,2]{1,2,0:T(2,128)}, u32[]{:S(2)}) copy-start(s32[1,128,2]{1,2,0:T(2,128)} %param.17) | copy-start | bytes 3076
  33.9 322.8 %copy-start.26 = (s32[1,128,2]{1,2,0:T(2,128)S(1)}, s32[1,128,2]{1,2,0:T(2,128)}, u32[]{:S(2)}) copy-start(s32[1,128,2]{1,2,0:T(2,128)} %param.18) | copy-start | bytes 3076
  33.9 383.7 %copy-start.34 = (u32[32]{0:T(128)S(1)}, u32[32]{0:T(128)}, u32[]{:S(2)}) copy-start(u32[32]{0:T(128)} %constant.53) | copy-start | bytes 388
  356.8 0.6 copy-start.20
  418.9 41.4 %copy-start.14 = (f32[4096]{0:T(1024)}, f32[4096]{0:T(1024)S(1)}, u32[]{:S(2)}) copy-start(f32[4096]{0:T(1024)S(1)} %get-tuple-element.37) | copy-start | bytes 49156
  419.0 245.5 %all-to-all-start.1 = ((bf16[2,704,2048]{2,1,0:T(8,128)(2,1)}), bf16[2,704,2048]{2,1,0:T(8,128)(2,1)}, u32[]{:S(2)}, u32[]{:S(2)}) async-start(bf16[2,704,2048]{2,1,0:T(8,128)(2,1)} %bitcast.154), calls=%async_computation.1 | async-start | bytes 11534336 | tf_op jit(solution)/shard_map/all_to_all | solution.py:855
  425.2 619.8 %all-reduce.10.cloned.1.call-start = ((), (), s32[]{:S(2)}) async-start(), calls=%async_computation.6 | async-start | bytes 131072
  460.3 8.1 copy-start.1
  468.4 85.5 %copy-start.7 = (bf16[1,128,2048]{2,1,0:T(8,128)(2,1)S(1)}, bf16[1,128,2048]{2,1,0:T(8,128)(2,1)}, u32[]{:S(2)}) copy-start(bf16[1,128,2048]{2,1,0:T(8,128)(2,1)} %param.14) | copy-start | bytes 1572868
  468.4 86.3 %copy-start.16 = (f32[2048]{0:T(1024)S(1)}, f32[2048]{0:T(1024)}, u32[]{:S(2)}) copy-start(f32[2048]{0:T(1024)} %param.20) | copy-start | bytes 24580
  553.9 0.8 copy-start.3
  554.7 97.8 %copy-start.30 = (f32[128]{0:T(128)}, f32[128]{0:T(128)S(1)}, u32[]{:S(2)}) copy-start(f32[128]{0:T(128)S(1)} %get-tuple-element.42) | copy-start | bytes 1540
  664.6 19.8 %copy-start.12 = (bf16[128,2048]{1,0:T(8,128)(2,1)S(1)}, bf16[128,2048]{1,0:T(8,128)(2,1)}, u32[]{:S(2)}) copy-start(bf16[128,2048]{1,0:T(8,128)(2,1)} %multiply_convert_fusion.6.x_ref) | copy-start | bytes 1572868
  664.6 19.8 %copy-start.23 = (bf16[2048,4]{0,1:T(4,128)(2,1)S(1)}, bf16[2048,4]{0,1:T(4,128)(2,1)}, u32[]{:S(2)}) copy-start(bf16[2048,4]{0,1:T(4,128)(2,1)} %param.22) | copy-start | bytes 49156
  766.8 11.6 copy-start.5
  766.8 12.5 copy-start.35
  787.5 609.7 %collective-permute-start.1 = (bf16[704,2048]{1,0:T(8,128)(2,1)}, bf16[704,2048]{1,0:T(8,128)(2,1)}, u32[]{:S(2)}, u32[]{:S(2)}) collective-permute-start(bf16[704,2048]{1,0:T(8,128)(2,1)} %convolution_convert_fusion.11), channel_id=1, source_target_pairs={{0,0},{4,1},{1,2},{5,3},{2,4},{6,5},{3,6},{7,7},{8,8},{12,9},{9,10... | collective-permute-start | bytes 8650760 | tf_op jit(solution)/shard_map/ppermute | solution.py:946
  801.5 10.5 copy-start.22
  962.0 84.4 %copy-start.4 = (bf16[128,2048]{1,0:T(8,128)(2,1)S(1)}, bf16[128,2048]{1,0:T(8,128)(2,1)}, u32[]{:S(2)}) copy-start(bf16[128,2048]{1,0:T(8,128)(2,1)} %copy-done.3) | copy-start | bytes 1572868
  962.0 84.4 %copy-start.8 = (bf16[1,128,2048]{2,1,0:T(8,128)(2,1)S(1)}, bf16[1,128,2048]{2,1,0:T(8,128)(2,1)}, u32[]{:S(2)}) copy-start(bf16[1,128,2048]{2,1,0:T(8,128)(2,1)} %param.14) | copy-start | bytes 1572868
  962.0 84.4 %copy-start.17 = (f32[2048]{0:T(1024)S(1)}, f32[2048]{0:T(1024)}, u32[]{:S(2)}) copy-start(f32[2048]{0:T(1024)} %param.20) | copy-start | bytes 24580
  962.0 84.4 %copy-start.31 = (f32[128]{0:T(128)S(1)}, f32[128]{0:T(128)}, u32[]{:S(2)}) copy-start(f32[128]{0:T(128)} %copy-done.30) | copy-start | bytes 1540
  962.0 85.9 %copy-start.33 = (f32[128]{0:T(128)S(1)}, f32[128]{0:T(128)}, u32[]{:S(2)}) copy-start(f32[128]{0:T(128)} %get-tuple-element.41) | copy-start | bytes 1540
  1179.1 75.9 %all-to-all-start.2 = ((bf16[8,256,768]{2,1,0:T(8,128)(2,1)}), bf16[8,256,768]{2,1,0:T(8,128)(2,1)}, u32[]{:S(2)}, u32[]{:S(2)}) async-start(bf16[8,256,768]{2,1,0:T(8,128)(2,1)} %bitcast.157), calls=%async_computation.2 | async-start | bytes 6291456 | tf_op jit(solution)/shard_map/all_to_all | solution.py:972
  1186.6 195.4 %all-reduce.12.cloned.1.call-start = ((), (), s32[]{:S(2)}) async-start(), calls=%async_computation.7 | async-start | bytes 131072
  1254.9 133.6 %all-to-all-start.3 = ((bf16[2,704,2048]{2,1,0:T(8,128)(2,1)}), bf16[2,704,2048]{2,1,0:T(8,128)(2,1)}, u32[]{:S(2)}, u32[]{:S(2)}) async-start(bf16[2,704,2048]{2,1,0:T(8,128)(2,1)} %bitcast.155), calls=%async_computation.3 | async-start | bytes 11534336 | tf_op jit(solution)/shard_map/all_to_all | solution.py:943
  1261.1 157.6 %all-reduce.8.cloned.1.call-start = ((), (), s32[]{:S(2)}) async-start(), calls=%async_computation.5 | async-start | bytes 4194304 | tf_op jit(solution)/shard_map/psum | solution.py:976
  1265.1 6.3 copy-start.2
  1265.1 6.3 copy-start.15
  1271.4 279.4 %all-reduce.14.cloned.1.call-start = ((), (), s32[]{:S(2)}) async-start(), calls=%async_computation.8 | async-start | bytes 163840 | tf_op jit(solution)/shard_map/psum | solution.py:984
  1283.2 97.9 %copy-start.13 = (bf16[128,2048]{1,0:T(8,128)(2,1)S(1)}, bf16[128,2048]{1,0:T(8,128)(2,1)}, u32[]{:S(2)}) copy-start(bf16[128,2048]{1,0:T(8,128)(2,1)} %multiply_convert_fusion.6.x_ref) | copy-start | bytes 1572868
  1283.2 100.1 %copy-start.21 = (f32[128,4]{0,1:T(4,128)S(1)}, f32[128,4]{0,1:T(4,128)}, u32[]{:S(2)}) copy-start(f32[128,4]{0,1:T(4,128)} %copy-done.20) | copy-start | bytes 6148
  1283.2 100.2 %copy-start.11 = (bf16[128,2048]{1,0:T(8,128)(2,1)S(1)}, bf16[128,2048]{1,0:T(8,128)(2,1)}, u32[]{:S(2)}) copy-start(bf16[128,2048]{1,0:T(8,128)(2,1)} %fusion.8.x_ref) | copy-start | bytes 1572868
  1283.2 101.1 %copy-start.9 = (bf16[1,128,2048]{2,1,0:T(8,128)(2,1)S(1)}, bf16[1,128,2048]{2,1,0:T(8,128)(2,1)}, u32[]{:S(2)}) copy-start(bf16[1,128,2048]{2,1,0:T(8,128)(2,1)} %param.14) | copy-start | bytes 1572868
  1283.2 101.1 %copy-start.19 = (f32[2048]{0:T(1024)S(1)}, f32[2048]{0:T(1024)}, u32[]{:S(2)}) copy-start(f32[2048]{0:T(1024)} %param.19) | copy-start | bytes 24580
  1283.2 101.1 %copy-start.25 = (bf16[2048,4]{0,1:T(4,128)(2,1)S(1)}, bf16[2048,4]{0,1:T(4,128)(2,1)}, u32[]{:S(2)}) copy-start(bf16[2048,4]{0,1:T(4,128)(2,1)} %param.21) | copy-start | bytes 49156
  1283.2 101.1 %copy-start.29 = (f32[128]{0:T(128)S(1)}, f32[128]{0:T(128)}, u32[]{:S(2)}) copy-start(f32[128]{0:T(128)} %copy-done.28) | copy-start | bytes 1540
  1283.2 102.6 %copy-start.32 = (f32[128]{0:T(128)S(1)}, f32[128]{0:T(128)}, u32[]{:S(2)}) copy-start(f32[128]{0:T(128)} %get-tuple-element.39) | copy-start | bytes 1540
Sparse Core Ops, SparseCore 0:
  11.6 245.9 all-gather.3
  812.7 152.3 all-reduce.9
  1207.7 147.0 all-reduce.11
  1357.6 60.9 all-reduce.7
  1425.2 125.5 all-reduce.13

commit v2 on v1

--- a/solution.py
+++ b/solution.py
@@ -1,3 +1,4 @@
+import functools
 import math
 
 import jax
@@ -421,251 +422,475 @@
 
 class Place:
     def __init__(self):
-        self.e = lax.axis_index("expert"); self.x = lax.axis_index("context"); self.z = lax.axis_index("dp")
+        self.e = lax.axis_index("expert")
+        self.x = lax.axis_index("context")
+        self.z = lax.axis_index("dp")
         self.own = (self.e, self.x)
         self.c = lax.rem(self.e, 2)
         self.sib = (self.e + 1 - 2 * self.c, self.x)
         self.cols = self.columns(self.e, self.x, self.c)
         self.sib_cols = self.columns(self.sib[0], self.x, 1 - self.c)
+
     def columns(self, e, x, c):
         first = (lax.rem(e + 2 * c, 4), lax.rem(x + 1 - c, 2))
         second = (lax.rem(e + 2 * (1 - c), 4), lax.rem(x + c, 2))
-        diag = (lax.rem(e + 2, 4), 1 - x)
-        return ((e, x), first, second, diag)
+        return ((e, x), first, second, (lax.rem(e + 2, 4), 1 - x))
+
     def dev(self, col, z=None):
         return (col[0], col[1], self.z if z is None else z)
+
     def block(self, col, z):
         return z * 8 + col[0] * 2 + col[1]
 
-def greet(pc, sides):
+
+def signal(barrier, dev):
+    pl.semaphore_signal(barrier, inc=1, device_id=dev, device_id_type=MESH)
+
+
+def greet(pc):
     barrier = pltpu.get_barrier_semaphore()
     for col in (pc.sib, pc.cols[1], pc.cols[2]):
-        pl.semaphore_signal(barrier, inc=1, device_id=pc.dev(col), device_id_type=MESH)
-    @pl.when(pc.z > 0)
-    def _():
-        pl.semaphore_signal(barrier, inc=1, device_id=pc.dev(pc.own, pc.z - 1), device_id_type=MESH)
-    @pl.when(pc.z < sides - 1)
-    def _():
-        pl.semaphore_signal(barrier, inc=1, device_id=pc.dev(pc.own, pc.z + 1), device_id_type=MESH)
-    pl.semaphore_wait(barrier, 3 + lax.div(pc.z + sides - 1, sides) + lax.div(2 * sides - 2 - pc.z, sides))
-
-
-def gather_kernel(x_ref, out_ref, loc, zs, zr, fs, fr, ss, sr, bs, br):
+        signal(barrier, pc.dev(col))
+    pl.when(pc.z > 0)(lambda: signal(barrier, pc.dev(pc.own, pc.z - 1)))
+    pl.when(pc.z < 3)(lambda: signal(barrier, pc.dev(pc.own, pc.z + 1)))
+    pl.semaphore_wait(barrier, 3 + lax.div(pc.z + 3, 4) + lax.div(6 - pc.z, 4))
+
+
+class Copies:
+    def __init__(self, parts):
+        self.parts = parts
+
+    def start(self):
+        for part in self.parts:
+            part.start()
+
+    def wait_send(self):
+        for part in self.parts:
+            part.wait_send()
+
+    def wait_recv(self):
+        for part in self.parts:
+            part.wait_recv()
+
+
+def remote(src, dst, send, recv, dev):
+    return pltpu.make_async_remote_copy(
+        src_ref=src, dst_ref=dst, send_sem=send, recv_sem=recv, device_id=dev, device_id_type=MESH
+    )
+
+
+def when_in(cond, run):
+    if cond is True:
+        run()
+    else:
+        pl.when(cond)(run)
+
+
+class Gather:
+    sems = ((), (2, 4), (2, 4), (7,), (7,), (2, 7), (2, 7), (4, 7), (4, 7))
+
+    def __init__(self, pc, ins, outs, sems):
+        self.pc, self.ins, self.outs = pc, ins, outs
+        self.loc, self.zs, self.zr, self.fs, self.fr, self.ss, self.sr, self.bs, self.br = sems
+
+    @classmethod
+    def scratch(cls, payloads):
+        return [pltpu.SemaphoreType.DMA((payloads,) + shape) for shape in cls.sems]
+
+    def copies(self, src_own, blk, send, recv, at, dev):
+        return Copies(
+            [
+                remote(
+                    self.ins[p] if src_own else self.outs[p].at[blk],
+                    self.outs[p].at[blk],
+                    send.at[(p,) + at],
+                    recv.at[(p,) + at],
+                    dev,
+                )
+                for p in range(len(self.ins))
+            ]
+        )
+
+    def hop(self, col, d, kind):
+        pc = self.pc
+        blk = pc.block(pc.cols[col], pc.z + d)
+        own = col == 0 and d == 0
+        if kind == "f":
+            return self.copies(own, blk, self.fs, self.fr, (d + 3,), pc.dev(pc.cols[1]))
+        if kind == "s":
+            return self.copies(own, blk, self.ss, self.sr, (col, d + 3), pc.dev(pc.cols[2]))
+        return self.copies(own, blk, self.bs, self.br, (col, d + 3), pc.dev(pc.sib))
+
+    def line(self, d, up):
+        pc = self.pc
+        dev = pc.dev(pc.own, pc.z + 1 if up else pc.z - 1)
+        blk = pc.block(pc.own, pc.z + d)
+        return self.copies(d == 0, blk, self.zs, self.zr, (0 if up else 1, abs(d)), dev)
+
+    def arrival(self, col, d, recv, at, dev):
+        blk = self.pc.block(col, self.pc.z + d)
+        return self.copies(False, blk, recv, recv, at, dev)
+
+    def present(self, d):
+        return True if d == 0 else (self.pc.z + d >= 0) & (self.pc.z + d <= 3)
+
+    def keep_own(self):
+        pc = self.pc
+        return [
+            pltpu.make_async_copy(
+                self.ins[p], self.outs[p].at[pc.block(pc.own, pc.z)], self.loc.at[p]
+            )
+            for p in range(len(self.ins))
+        ]
+
+    def start(self):
+        for copy in self.keep_own():
+            copy.start()
+
+    def own_line(self, d):
+        pc = self.pc
+
+        def run():
+            if d < 0:
+                below = pc.dev(pc.own, pc.z - 1)
+                self.arrival(pc.own, d, self.zr, (0, -d - 1), below).wait_recv()
+            if d > 0:
+                above = pc.dev(pc.own, pc.z + 1)
+                self.arrival(pc.own, d, self.zr, (1, d - 1), above).wait_recv()
+            if d <= 0:
+                pl.when(pc.z < 3)(lambda: self.line(d, True).start())
+            if d >= 0:
+                pl.when(pc.z > 0)(lambda: self.line(d, False).start())
+            for kind in ("f", "s", "b"):
+                self.hop(0, d, kind).start()
+
+        when_in(self.present(d), run)
+
+    def first_col(self, d):
+        pc = self.pc
+
+        def run():
+            self.arrival(pc.cols[1], d, self.fr, (d + 3,), pc.dev(pc.cols[1])).wait_recv()
+            self.hop(1, d, "s").start()
+            self.hop(1, d, "b").start()
+
+        when_in(self.present(d), run)
+
+    def last_cols(self, d):
+        pc = self.pc
+
+        def run():
+            for col, sent in ((2, 0), (3, 1)):
+                dev = pc.dev(pc.cols[2])
+                self.arrival(pc.cols[col], d, self.sr, (sent, d + 3), dev).wait_recv()
+                self.hop(col, d, "b").start()
+
+        when_in(self.present(d), run)
+
+    def finish(self, d):
+        pc = self.pc
+
+        def run():
+            for col in range(4):
+                dev = pc.dev(pc.sib)
+                self.arrival(pc.sib_cols[col], d, self.br, (col, d + 3), dev).wait_recv()
+            self.hop(0, d, "f").wait_send()
+            for col in (0, 1):
+                self.hop(col, d, "s").wait_send()
+            for col in range(4):
+                self.hop(col, d, "b").wait_send()
+            if d <= 0:
+                pl.when(pc.z < 3)(lambda: self.line(d, True).wait_send())
+            if d >= 0:
+                pl.when(pc.z > 0)(lambda: self.line(d, False).wait_send())
+
+        when_in(self.present(d), run)
+
+    def end(self):
+        for copy in self.keep_own():
+            copy.wait()
+
+    def events(self):
+        steps = [(self.own_line, 0)]
+        for s in (1, 2, 3):
+            steps += [(self.own_line, -s), (self.own_line, s)]
+            steps += [(self.first_col, d) for d in sorted({1 - s, s - 1})]
+        steps += [(self.first_col, -3), (self.first_col, 3)]
+        order = (0, -1, 1, -2, 2, -3, 3)
+        steps += [(self.last_cols, d) for d in order] + [(self.finish, d) for d in order]
+        return [lambda run=run, d=d: run(d) for run, d in steps]
+
+
+def gather_kernel(count, *refs):
+    pc = Place()
+    gather = Gather(pc, refs[:count], refs[count : 2 * count], refs[2 * count :])
+    gather.start()
+    greet(pc)
+    for event in gather.events():
+        event()
+    gather.end()
+
+
+def gather_all(blocks, cid):
+    count = len(blocks)
+    return pl.pallas_call(
+        functools.partial(gather_kernel, count),
+        out_shape=[jax.ShapeDtypeStruct((32,) + b.shape, b.dtype) for b in blocks],
+        in_specs=[pl.BlockSpec(memory_space=pltpu.VMEM)] * count,
+        out_specs=[pl.BlockSpec(memory_space=pl.ANY)] * count,
+        scratch_shapes=Gather.scratch(count),
+        compiler_params=pltpu.CompilerParams(collective_id=cid, has_side_effects=True),
+        name="gather_all",
+    )(*blocks)
+
+
+class Scatter:
+    sems = ((4, 4), (4, 4), (4, 4), (4, 2), (4, 2), (4,), (4,), (2, 4), (2, 4))
+
+    def __init__(self, pc, ins, bufs, sems):
+        self.pc, self.ins = pc, ins
+        count = len(ins)
+        self.acc, self.sib, self.sec, self.fst, self.zin = (
+            bufs[i * count : (i + 1) * count] for i in range(5)
+        )
+        self.ld, self.bs, self.br, self.ss, self.sr, self.fs, self.fr, self.zs, self.zr = sems
+        inner = lax.rem(lax.div(pc.z + 1, 2), 2)
+        low = 1 - lax.div(pc.z, 2)
+
+        def group(k):
+            v = (1 - inner) * k + inner * (0, 1, 3, 2)[k]
+            return low * (3 - v) + (1 - low) * v
+
+        self.group = group
+
+    @classmethod
+    def scratch(cls, blocks):
+        bufs = []
+        for lead in ((4, 4), (4, 4), (4, 2), (4,), (2, 4)):
+            bufs += [pltpu.VMEM(lead + shape, dtype) for shape, dtype in blocks]
+        return bufs + [pltpu.SemaphoreType.DMA((len(blocks),) + s) for s in cls.sems]
+
+    def copies(self, src, dst, send, recv, sent_at, got_at, dev):
+        return Copies(
+            [
+                remote(src(p), dst(p), send.at[(p,) + sent_at], recv.at[(p,) + got_at], dev)
+                for p in range(len(self.ins))
+            ]
+        )
+
+    def loads(self, k, col):
+        pc = self.pc
+        blk = pc.block(pc.cols[col], self.group(k))
+        return [
+            pltpu.make_async_copy(self.ins[p].at[blk], self.acc[p].at[k, col], self.ld.at[p, k, col])
+            for p in range(len(self.ins))
+        ]
+
+    def to_sib(self, k, col):
+        pc = self.pc
+        blk = pc.block(pc.sib_cols[col], self.group(k))
+        return self.copies(
+            lambda p: self.ins[p].at[blk], lambda p: self.sib[p].at[k, col],
+            self.bs, self.br, (k, col), (k, col), pc.dev(pc.sib),
+        )
+
+    def to_second(self, k, j):
+        pc = self.pc
+        return self.copies(
+            lambda p: self.acc[p].at[k, 2 + j], lambda p: self.sec[p].at[k, j],
+            self.ss, self.sr, (k, j), (k, j), pc.dev(pc.cols[2]),
+        )
+
+    def to_first(self, k):
+        pc = self.pc
+        return self.copies(
+            lambda p: self.acc[p].at[k, 1], lambda p: self.fst[p].at[k],
+            self.fs, self.fr, (k,), (k,), pc.dev(pc.cols[1]),
+        )
+
+    def to_z(self, k, up):
+        pc, g, i = self.pc, self.group(k), 0 if up else 1
+        return self.copies(
+            lambda p: self.acc[p].at[k, 0], lambda p: self.zin[p].at[i, g],
+            self.zs, self.zr, (i, k), (i, g), pc.dev(pc.own, pc.z + 1 if up else pc.z - 1),
+        )
+
+    def from_z(self, g, i):
+        pc = self.pc
+        return self.copies(
+            lambda p: self.acc[p].at[0, 0], lambda p: self.zin[p].at[i, g],
+            self.zs, self.zr, (i, 0), (i, g), pc.dev(pc.own, pc.z - 1 if i == 0 else pc.z + 1),
+        )
+
+    def add(self, k, col, others):
+        for acc, other in zip(self.acc, others):
+            rows, step = acc.shape[2], min(16, acc.shape[2])
+
+            def body(i, carry, acc=acc, other=other, step=step):
+                r = pl.ds(pl.multiple_of(i * step, step), step)
+                both = acc[k, col, r, :].astype(jnp.float32) + other[r, :].astype(jnp.float32)
+                acc[k, col, r, :] = both.astype(acc.dtype)
+                return carry
+
+            lax.fori_loop(0, rows // step, body, 0)
+
+    def start_loads(self):
+        for k in range(4):
+            for col in (2, 3, 1, 0):
+                for copy in self.loads(k, col):
+                    copy.start()
+
+    def start(self):
+        for k in range(4):
+            for col in (2, 3, 1, 0):
+                self.to_sib(k, col).start()
+
+    def join(self, k, col):
+        for copy in self.loads(k, col):
+            copy.wait()
+        self.to_sib(k, col).wait_recv()
+        self.add(k, col, [buf.at[k, col] for buf in self.sib])
+
+    def stage_a(self, k):
+        for j in (0, 1):
+            self.join(k, 2 + j)
+            self.to_second(k, j).start()
+
+    def stage_b(self, k):
+        self.join(k, 1)
+        self.to_second(k, 1).wait_recv()
+        self.add(k, 1, [buf.at[k, 1] for buf in self.sec])
+        self.to_first(k).start()
+        self.join(k, 0)
+
+    def stage_c(self, k):
+        z = self.pc.z
+        self.to_second(k, 0).wait_recv()
+        self.add(k, 0, [buf.at[k, 0] for buf in self.sec])
+        self.to_first(k).wait_recv()
+        self.add(k, 0, [buf.at[k] for buf in self.fst])
+        g = self.group(k)
+
+        def arrive(i):
+            self.from_z(g, i).wait_recv()
+            self.add(k, 0, [buf.at[i, g] for buf in self.zin])
+
+        def upward():
+            pl.when(z > 0)(lambda: arrive(0))
+            self.to_z(k, True).start()
+
+        def downward():
+            pl.when(z < 3)(lambda: arrive(1))
+            self.to_z(k, False).start()
+
+        if k < 3:
+            pl.when(g > z)(upward)
+            pl.when(g < z)(downward)
+        else:
+            pl.when(z > 0)(lambda: arrive(0))
+            pl.when(z < 3)(lambda: arrive(1))
+
+    def events(self):
+        a, b, c = self.stage_a, self.stage_b, self.stage_c
+        steps = [(a, 0), (a, 1), (b, 0), (a, 2), (b, 1), (c, 0), (a, 3), (b, 2), (c, 1), (b, 3)]
+        return [lambda run=run, k=k: run(k) for run, k in steps + [(c, 2), (c, 3)]]
+
+    def end(self):
+        z = self.pc.z
+        for k in range(4):
+            for col in range(4):
+                self.to_sib(k, col).wait_send()
+            for j in (0, 1):
+                self.to_second(k, j).wait_send()
+            self.to_first(k).wait_send()
+            if k < 3:
+                pl.when(self.group(k) > z)(lambda: self.to_z(k, True).wait_send())
+                pl.when(self.group(k) < z)(lambda: self.to_z(k, False).wait_send())
+
+
+def scatter_kernel(count, *refs):
+    pc = Place()
+    outs = refs[count : 2 * count]
+    scatter = Scatter(pc, refs[:count], refs[2 * count : 7 * count], refs[7 * count :])
+    scatter.start_loads()
+    greet(pc)
+    scatter.start()
+    for event in scatter.events():
+        event()
+    for p in range(count):
+        outs[p][...] = scatter.acc[p][3, 0]
+    scatter.end()
+
+
+def scatter_all(wholes, cid):
+    count = len(wholes)
+    blocks = [(w.shape[1:], w.dtype) for w in wholes]
+    return pl.pallas_call(
+        functools.partial(scatter_kernel, count),
+        out_shape=[jax.ShapeDtypeStruct(*b) for b in blocks],
+        in_specs=[pl.BlockSpec(memory_space=pl.ANY)] * count,
+        out_specs=[pl.BlockSpec(memory_space=pltpu.VMEM)] * count,
+        scratch_shapes=Scatter.scratch(blocks),
+        compiler_params=pltpu.CompilerParams(
+            collective_id=cid, has_side_effects=True, vmem_limit_bytes=48 << 20
+        ),
+        name="scatter_all",
+    )(*wholes)
+
+
+def sum_kernel(v_ref, out_ref, cur, got, lines, send, recv, zsend, zrecv):
     pc = Place()
     z = pc.z
-    mine = pltpu.make_async_copy(x_ref, out_ref.at[pc.block(pc.own, z)], loc)
-    mine.start()
-    greet(pc, 4)
-    def rc(src, blk, s, r, dev):
-        return pltpu.make_async_remote_copy(src_ref=src, dst_ref=out_ref.at[blk], send_sem=s, recv_sem=r, device_id=dev, device_id_type=MESH)
-    def hop(col, d, kind):
-        zz = z + d
-        blk = pc.block(pc.cols[col], zz)
-        src = x_ref if (col == 0 and d == 0) else out_ref.at[blk]
-        i = d + 3
-        if kind == "f":
-            return rc(src, blk, fs.at[i], fr.at[i], pc.dev(pc.cols[1]))
-        if kind == "s":
-            return rc(src, blk, ss.at[col, i], sr.at[col, i], pc.dev(pc.cols[2]))
-        return rc(src, blk, bs.at[col, i], br.at[col, i], pc.dev(pc.sib))
-    def zhop(d, up):
-        zz = z + d
-        blk = pc.block(pc.own, zz)
-        src = x_ref if d == 0 else out_ref.at[blk]
-        i = 0 if up else 1
-        return rc(src, blk, zs.at[i, abs(d)], zr.at[i, abs(d)], pc.dev(pc.own, z + 1 if up else z - 1))
-    def ok(d):
-        return (z + d >= 0) & (z + d <= 3)
-    def when(cond, f):
-        if cond is True:
-            f()
-        else:
-            pl.when(cond)(f)
-    def start_z(d):
-        if d <= 0:
-            pl.when(ok(d) & (z < 3))(lambda: zhop(d, True).start())
-        if d >= 0:
-            pl.when(ok(d) & (z > 0))(lambda: zhop(d, False).start())
-    def own_line(d):
-        def go():
-            if d < 0:
-                rc(out_ref.at[0], pc.block(pc.own, z + d), zs.at[0, -d - 1], zr.at[0, -d - 1], pc.dev(pc.own)).wait_recv()
-            if d > 0:
-                rc(out_ref.at[0], pc.block(pc.own, z + d), zs.at[1, d - 1], zr.at[1, d - 1], pc.dev(pc.own)).wait_recv()
-            if d <= 0:
-                pl.when(z < 3)(lambda: zhop(d, True).start())
-            if d >= 0:
-                pl.when(z > 0)(lambda: zhop(d, False).start())
-            hop(0, d, "f").start()
-            hop(0, d, "s").start()
-            hop(0, d, "b").start()
-        when(True if d == 0 else ok(d), go)
-    def first_col(d):
-        def go():
-            blk = pc.block(pc.cols[1], z + d)
-            rc(out_ref.at[0], blk, fs.at[d + 3], fr.at[d + 3], pc.dev(pc.own)).wait_recv()
-            hop(1, d, "s").start()
-            hop(1, d, "b").start()
-        when(True if d == 0 else ok(d), go)
-    def last_cols(d):
-        def go():
-            for col, j in ((2, 0), (3, 1)):
-                blk = pc.block(pc.cols[col], z + d)
-                rc(out_ref.at[0], blk, ss.at[j, d + 3], sr.at[j, d + 3], pc.dev(pc.own)).wait_recv()
-                hop(col, d, "b").start()
-        when(True if d == 0 else ok(d), go)
-    own_line(0)
-    for s in (1, 2, 3):
-        own_line(-s); own_line(s)
-        if s == 1:
-            first_col(0)
-        else:
-            first_col(-(s - 1)); first_col(s - 1)
-    first_col(-3); first_col(3)
-    for d in (0, -1, 1, -2, 2, -3, 3):
-        last_cols(d)
-    for d in (0, -1, 1, -2, 2, -3, 3):
-        def go():
-            for j in range(4):
-                blk = pc.block(pc.sib_cols[j], z + d)
-                rc(out_ref.at[0], blk, bs.at[j, d + 3], br.at[j, d + 3], pc.dev(pc.own)).wait_recv()
-            hop(0, d, "f").wait_send()
-            for col in (0, 1):
-                hop(col, d, "s").wait_send()
-            for col in range(4):
-                hop(col, d, "b").wait_send()
-            if d <= 0:
-                pl.when(z < 3)(lambda: zhop(d, True).wait_send())
-            if d >= 0:
-                pl.when(z > 0)(lambda: zhop(d, False).wait_send())
-        when(True if d == 0 else ok(d), go)
-    mine.wait()
-
-def gather_all(x, cid):
-    rows, width = x.shape
+    near = (pc.sib, (pc.e, 1 - pc.x), (lax.rem(pc.e + 2, 4), pc.x))
+    barrier = pltpu.get_barrier_semaphore()
+    for col in near:
+        signal(barrier, pc.dev(col))
+    for d in (1, 2, 3):
+        signal(barrier, pc.dev(pc.own, lax.rem(z + d, 4)))
+    pl.semaphore_wait(barrier, 6)
+    for s, col in enumerate(near):
+        src = v_ref if s == 0 else cur.at[s - 1]
+        copy = remote(src, got.at[s], send.at[s], recv.at[s], pc.dev(col))
+        copy.start()
+        copy.wait_recv()
+        cur[s] = src[...] + got[s]
+
+    def along(d):
+        there = lax.rem(z + d, 4)
+        return remote(cur.at[2], lines.at[z], zsend.at[d], zrecv.at[z], pc.dev(pc.own, there))
+
+    for d in (1, 2, 3):
+        along(d).start()
+    for d in (1, 2, 3):
+        source = lax.rem(z + d, 4)
+        remote(
+            cur.at[2], lines.at[source], zsend.at[0], zrecv.at[source], pc.dev(pc.own, source)
+        ).wait_recv()
+    lines[z] = cur[2]
+    out_ref[...] = ((lines[0] + lines[1]) + lines[2]) + lines[3]
+    for s, col in enumerate(near):
+        src = v_ref if s == 0 else cur.at[s - 1]
+        remote(src, got.at[s], send.at[s], recv.at[s], pc.dev(col)).wait_send()
+    for d in (1, 2, 3):
+        along(d).wait_send()
+
+
+def sum_all(v, cid):
     D = pltpu.SemaphoreType.DMA
-    out = pl.pallas_call(
-        gather_kernel,
-        out_shape=jax.ShapeDtypeStruct((32, rows, width), x.dtype),
+    return pl.pallas_call(
+        sum_kernel,
+        out_shape=jax.ShapeDtypeStruct(v.shape, v.dtype),
         in_specs=[pl.BlockSpec(memory_space=pltpu.VMEM)],
-        out_specs=pl.BlockSpec(memory_space=pl.ANY),
-        scratch_shapes=[D, D((2, 4)), D((2, 4)), D((7,)), D((7,)), D((2, 7)), D((2, 7)), D((4, 7)), D((4, 7))],
+        out_specs=pl.BlockSpec(memory_space=pltpu.VMEM),
+        scratch_shapes=[
+            pltpu.VMEM((3,) + v.shape, v.dtype),
+            pltpu.VMEM((3,) + v.shape, v.dtype),
+            pltpu.VMEM((4,) + v.shape, v.dtype),
+            D((3,)), D((3,)), D((4,)), D((4,)),
+        ],
         compiler_params=pltpu.CompilerParams(collective_id=cid, has_side_effects=True),
-        name="gather_all",
-    )(x)
-    return out.reshape(32 * rows, width)
-
-def scatter_kernel(p_ref, out_ref, acc, sib, sec, fst, zin, ld, bs, br, ss, sr, fs, fr, zs, zr):
-    pc = Place()
-    z = pc.z
-    rows = p_ref.shape[1]
-    inner = lax.rem(lax.div(z + 1, 2), 2)
-    low = 1 - lax.div(z, 2)
-    gray = (0, 1, 3, 2)
-    def group(k):
-        v = (1 - inner) * k + inner * gray[k]
-        return low * (3 - v) + (1 - low) * v
-    def rc(src, dst, s, r, dev):
-        return pltpu.make_async_remote_copy(src_ref=src, dst_ref=dst, send_sem=s, recv_sem=r, device_id=dev, device_id_type=MESH)
-    def load(k, col):
-        return pltpu.make_async_copy(p_ref.at[pc.block(pc.cols[col], group(k))], acc.at[k, col], ld.at[k, col])
-    def to_sib(k, col):
-        return rc(p_ref.at[pc.block(pc.sib_cols[col], group(k))], sib.at[k, col], bs.at[k, col], br.at[k, col], pc.dev(pc.sib))
-    def to_second(k, j):
-        return rc(acc.at[k, 2 + j], sec.at[k, j], ss.at[k, j], sr.at[k, j], pc.dev(pc.cols[2]))
-    def to_first(k):
-        return rc(acc.at[k, 1], fst.at[k], fs.at[k], fr.at[k], pc.dev(pc.cols[1]))
-    def to_z(k, up):
-        g = group(k)
-        i = 0 if up else 1
-        return rc(acc.at[k, 0], zin.at[i, g], zs.at[i, k], zr.at[i, g], pc.dev(pc.own, z + 1 if up else z - 1))
-    def from_z(g, i):
-        return rc(acc.at[0, 0], zin.at[i, g], zs.at[i, 0], zr.at[i, g], pc.dev(pc.own))
-    step = 16
-    def add(k, col, other):
-        def body(i, carry):
-            r = pl.ds(pl.multiple_of(i * step, step), step)
-            acc[k, col, r, :] = (acc[k, col, r, :].astype(jnp.float32) + other[r, :].astype(jnp.float32)).astype(acc.dtype)
-            return carry
-        lax.fori_loop(0, rows // step, body, 0)
-    for k in range(4):
-        for col in (2, 3, 1, 0):
-            load(k, col).start()
-    greet(pc, 4)
-    for k in range(4):
-        for col in (2, 3, 1, 0):
-            to_sib(k, col).start()
-    def join(k, col):
-        load(k, col).wait()
-        to_sib(k, col).wait_recv()
-        add(k, col, sib.at[k, col])
-    def stage_a(k):
-        for j in (0, 1):
-            join(k, 2 + j)
-            to_second(k, j).start()
-    def stage_b(k):
-        join(k, 1)
-        to_second(k, 1).wait_recv()
-        add(k, 1, sec.at[k, 1])
-        to_first(k).start()
-        join(k, 0)
-    def stage_c(k):
-        to_second(k, 0).wait_recv()
-        add(k, 0, sec.at[k, 0])
-        to_first(k).wait_recv()
-        add(k, 0, fst.at[k])
-        g = group(k)
-        if k < 3:
-            @pl.when(g > z)
-            def _():
-                @pl.when(z > 0)
-                def _():
-                    from_z(g, 0).wait_recv()
-                    add(k, 0, zin.at[0, g])
-                to_z(k, True).start()
-            @pl.when(g < z)
-            def _():
-                @pl.when(z < 3)
-                def _():
-                    from_z(g, 1).wait_recv()
-                    add(k, 0, zin.at[1, g])
-                to_z(k, False).start()
-        else:
-            @pl.when(z > 0)
-            def _():
-                from_z(z, 0).wait_recv()
-                add(k, 0, zin.at[0, z])
-            @pl.when(z < 3)
-            def _():
-                from_z(z, 1).wait_recv()
-                add(k, 0, zin.at[1, z])
-    stage_a(0); stage_a(1); stage_b(0); stage_a(2); stage_b(1); stage_c(0)
-    stage_a(3); stage_b(2); stage_c(1); stage_b(3); stage_c(2); stage_c(3)
-    out_ref[...] = acc[3, 0]
-    for k in range(4):
-        for col in range(4):
-            to_sib(k, col).wait_send()
-        for j in (0, 1):
-            to_second(k, j).wait_send()
-        to_first(k).wait_send()
-        if k < 3:
-            pl.when(group(k) > z)(lambda: to_z(k, True).wait_send())
-            pl.when(group(k) < z)(lambda: to_z(k, False).wait_send())
-
-def scatter_all(p, cid):
-    total, width = p.shape
-    rows = total // 32
-    D = pltpu.SemaphoreType.DMA
-    V = lambda *s: pltpu.VMEM(s + (rows, width), p.dtype)
-    return pl.pallas_call(
-        scatter_kernel,
-        out_shape=jax.ShapeDtypeStruct((rows, width), p.dtype),
-        in_specs=[pl.BlockSpec(memory_space=pl.ANY)],
-        out_specs=pl.BlockSpec(memory_space=pltpu.VMEM),
-        scratch_shapes=[V(4, 4), V(4, 4), V(4, 2), V(4), V(2, 4), D((4, 4)), D((4, 4)), D((4, 4)), D((4, 2)), D((4, 2)), D((4,)), D((4,)), D((2, 4)), D((2, 4))],
-        compiler_params=pltpu.CompilerParams(collective_id=cid, has_side_effects=True, vmem_limit_bytes=48 << 20),
-        name="scatter_all",
-    )(p.reshape(32, rows, width))
+        name="sum_all",
+    )(v)
 
 
 def attend_kernel(qkv_ref, att_ref, lse_ref):
@@ -796,17 +1021,14 @@
     )(qkv, du, lse, gate)
 
 
-def spread(per_token):
-    columns = per_token.T.reshape(1, -1)
-    whole = lax.all_gather(columns, EVERY, axis=0, tiled=True)
-    return whole.reshape(whole.shape[0], per_token.shape[1], per_token.shape[0])
-
-
-def home_sums(per_expert, experts):
-    devices, tokens = per_expert.shape
-    mine = (jnp.arange(experts) == lax.axis_index("expert")).astype(jnp.float32)
-    columns = (per_expert[:, None, :] * mine[None, :, None]).reshape(devices, experts * tokens)
-    return lax.psum_scatter(columns, EVERY, scatter_dimension=0, tiled=True).reshape(experts, tokens).T
+def as_rows(*columns):
+    rows = jnp.concatenate([c.T for c in columns], axis=0)
+    return jnp.pad(rows, ((0, -rows.shape[0] % 8), (0, 0)))
+
+
+def expert_rows(per_block, experts):
+    place = (jnp.arange(8) == lax.axis_index("expert")).astype(per_block.dtype)
+    return per_block[:, None, :] * place[None, :, None]
 
 
 def placed_weights(
@@ -852,12 +1074,7 @@
     w_qkv = lax.all_to_all(
         qkv_parts.reshape(-1, shares * piece), SHARE, split_axis=1, concat_axis=0, tiled=True
     )
-    w_pair = lax.all_to_all(w_in[0], "context", split_axis=0, concat_axis=0, tiled=True)
-    moves = [(s, (s % contexts) * slots + s // contexts) for s in range(shares)]
-    w_unit = lax.ppermute(w_down[0], SHARE, moves)
-    units = w_unit.shape[0]
-
-    all_one = gather_all(normed_one, 0)
+
     shares_a, picked_a = pair_gates(
         jnp.dot(normed_one, attn_router, preferred_element_type=f32), attn_routes[0], live, experts
     )
@@ -865,30 +1082,36 @@
     named_f = jnp.sum(
         (ffn_routes[0][:, :, None] == jnp.arange(experts, dtype=jnp.int32)).astype(f32), axis=1
     )
-    aux = lax.dynamic_index_in_dim(
-        spread(jnp.concatenate([gates_a, named_f * live[:, None]], axis=1)).reshape(
-            devices, 2, experts, tokens
-        ),
-        own_expert,
-        axis=2,
-        keepdims=False,
-    )
-    gate_a, named = aux[:, 0], aux[:, 1]
-    all_grad = lax.all_gather(grad_out.astype(low), EVERY, axis=0, tiled=True)
+    named_f = named_f * live[:, None]
+    all_one, aux = gather_all([normed_one, as_rows(gates_a, named_f)], 0)
+    all_one = all_one.reshape(-1, width)
+    gate_a = lax.dynamic_index_in_dim(aux, own_expert, axis=1, keepdims=False)
+    named = lax.dynamic_index_in_dim(aux, experts + own_expert, axis=1, keepdims=False)
+    all_one, own_in, own_down = lax.optimization_barrier((all_one, w_in[0], w_down[0]))
+    w_pair = lax.all_to_all(own_in, "context", split_axis=0, concat_axis=0, tiled=True)
+    share = lax.axis_index(SHARE)
+    moves = [(s, (s % contexts) * slots + s // contexts) for s in range(shares)]
+    stays = functools.reduce(jnp.logical_or, [share == s for s, d in moves if s == d])
+    w_unit = lax.ppermute(own_down, SHARE, [(s, d) for s, d in moves if s != d])
+    w_unit = jnp.where(stays, own_down, w_unit)
+    units = w_unit.shape[0]
     qkv = jnp.dot(all_one, w_qkv, preferred_element_type=f32).astype(low)
     attended, lse = attend(qkv, slots)
     gated = (attended.astype(f32) * gate_a.reshape(-1, 1)).astype(low)
     h1_part = jnp.dot(gated, w_out[0], preferred_element_type=f32).astype(low)
-    residual_one = x_float + scatter_all(h1_part, 1).astype(f32)
+    (h1_sum,) = scatter_all([h1_part.reshape(devices, tokens, width)], 1)
+    residual_one = x_float + h1_sum.astype(f32)
 
     scale_two = rms_scale(residual_one)
     normed_two = (residual_one * scale_two * norm2_gain).astype(low)
-    all_two = gather_all(normed_two, 2)
     shares_f, picked_f = pair_gates(
         jnp.dot(normed_two, ffn_router, preferred_element_type=f32), ffn_routes[0], live, experts
     )
     gates_f = jnp.sum(shares_f[:, :, None] * picked_f, axis=1)
-    gate_f = lax.dynamic_index_in_dim(spread(gates_f), own_expert, axis=1, keepdims=False)
+    all_two, aux = gather_all([normed_two, as_rows(gates_f)], 2)
+    gate_f = lax.dynamic_index_in_dim(aux, own_expert, axis=1, keepdims=False)
+    all_two, grad_low = lax.optimization_barrier((all_two, grad_out.astype(low)))
+    (all_grad,) = gather_all([grad_low], 7)
     earlier = (jnp.arange(tokens)[:, None] < jnp.arange(tokens)[None, :]).astype(f32)
     rank = jnp.dot(named, earlier, preferred_element_type=f32)
     table = jnp.where(
@@ -900,7 +1123,7 @@
         rows = jnp.einsum(
             "bst,btd->bsd",
             low_table,
-            whole.reshape(devices, tokens, width),
+            whole,
             preferred_element_type=f32,
         )
         return rows.astype(low).reshape(devices * room, width)
@@ -909,7 +1132,7 @@
         whole = jnp.einsum(
             "bst,bsd->btd", low_table, rows.reshape(devices, room, width), preferred_element_type=f32
         )
-        return whole.astype(low).reshape(devices * tokens, width)
+        return whole.astype(low)
 
     row_gate = jnp.sum(table * gate_f[:, None, :], axis=2).reshape(-1, 1)
     routed = pick(all_two)
@@ -919,13 +1142,13 @@
     hidden_f = gate_part * sigmoid_gate * up_part
     hidden = hidden_f.astype(low)
     down = (jnp.dot(hidden, w_unit, preferred_element_type=f32) * row_gate).astype(low)
-    mixed = scatter_all(put(down), 3).astype(f32)
-    layer_output = (live[:, None] * (residual_one + mixed)).astype(low)
+    (mixed,) = scatter_all([put(down)], 3)
+    layer_output = (live[:, None] * (residual_one + mixed.astype(f32))).astype(low)
 
     d_rows = pick(all_grad)
     d_plain = lax.dot_general(d_rows, w_unit, (((1,), (1,)), ((), ())), preferred_element_type=f32)
     row_sums = jnp.sum(d_plain * hidden.astype(f32), axis=1).reshape(devices, room)
-    dgate_f = home_sums(jnp.sum(table * row_sums[:, :, None], axis=1), experts)
+    dgate_part = expert_rows(jnp.sum(table * row_sums[:, :, None], axis=1), experts)
     d_hidden = d_plain * row_gate
     d_gate = d_hidden * up_part * sigmoid_gate * (1.0 + gate_part * (1.0 - sigmoid_gate))
     d_up = d_hidden * gate_part * sigmoid_gate
@@ -943,16 +1166,20 @@
     grad_w_in = lax.all_to_all(
         grad_pair.astype(low), "context", split_axis=0, concat_axis=0, tiled=True
     ).astype(f32)
-    grad_w_down = lax.ppermute(grad_unit.astype(low), SHARE, [(b, a) for a, b in moves]).astype(f32)
+    grad_moved = lax.ppermute(grad_unit.astype(low), SHARE, [(d, s) for s, d in moves if s != d])
+    grad_w_down = jnp.where(stays, grad_unit.astype(low), grad_moved).astype(f32)
+    d_two_sum, dgate_f = scatter_all([d_two_part, dgate_part], 4)
+    dgate_f = dgate_f[:experts].T
     dlog_f = gates_f * (dgate_f - jnp.sum(gates_f * dgate_f, axis=1, keepdims=True))
-    d_normed_two = scatter_all(d_two_part, 4).astype(f32) + jnp.dot(
+    d_normed_two = d_two_sum.astype(f32) + jnp.dot(
         dlog_f, ffn_router.astype(f32).T, precision=PRECISE
     )
-    local_ffn_router = jnp.dot(normed_two.astype(f32).T, dlog_f, precision=PRECISE)
+    local_ffn_router = jnp.dot(dlog_f.T, normed_two.astype(f32), precision=PRECISE)
     d_mid, local_gain_two = norm_back(residual_one, scale_two, norm2_gain, d_normed_two)
     d_residual = grad_out + d_mid
 
-    all_mid = gather_all(d_residual.astype(low), 5)
+    (all_mid,) = gather_all([d_residual.astype(low)], 5)
+    all_mid = all_mid.reshape(-1, width)
     d_att = lax.dot_general(
         all_mid, w_out[0], (((1,), (1,)), ((), ())), preferred_element_type=f32
     ).astype(low)
@@ -962,7 +1189,7 @@
     grad_w_out = lax.dot_general(
         gated, all_mid, (((0,), (0,)), ((), ())), preferred_element_type=f32
     )
-    dgate_a = home_sums(jnp.sum(head_sums, axis=1).reshape(devices, tokens), experts)
+    dgate_part = expert_rows(jnp.sum(head_sums, axis=1).reshape(devices, tokens), experts)
     d_one_part = lax.dot_general(
         d_qkv, w_qkv, (((1,), (1,)), ((), ())), preferred_element_type=f32
     ).astype(low)
@@ -974,17 +1201,23 @@
     grad_w_query = grad_parts[:, :, : QD // shares].reshape(-1, QD).astype(f32)
     kv_grads = grad_parts[:, :, QD // shares :].reshape(-1, shares, 2, QD // shares)
     grad_w_kv = lax.psum(kv_grads.transpose(0, 2, 1, 3).reshape(-1, 2 * QD), "expert").astype(f32)
+    d_one_sum, dgate_a = scatter_all([d_one_part.reshape(devices, tokens, width), dgate_part], 6)
+    dgate_a = dgate_a[:experts].T
     dlog_a = gates_a * (dgate_a - jnp.sum(gates_a * dgate_a, axis=1, keepdims=True))
-    d_normed_one = scatter_all(d_one_part, 6).astype(f32) + jnp.dot(
+    d_normed_one = d_one_sum.astype(f32) + jnp.dot(
         dlog_a, attn_router.astype(f32).T, precision=PRECISE
     )
-    local_attn_router = jnp.dot(normed_one.astype(f32).T, dlog_a, precision=PRECISE)
+    local_attn_router = jnp.dot(dlog_a.T, normed_one.astype(f32), precision=PRECISE)
     d_first, local_gain_one = norm_back(x_float, scale_one, norm1_gain, d_normed_one)
     input_grad = d_residual + d_first
-    gain_one_sum, gain_two_sum, router_a_sum, router_f_sum = lax.psum(
-        (local_gain_one, local_gain_two, local_attn_router, local_ffn_router),
-        ("expert", "context", "dp"),
-    )
+    sums = sum_all(
+        jnp.concatenate(
+            [local_gain_one[None], local_gain_two[None], local_attn_router, local_ffn_router]
+        ).reshape(-1, HEAD_DIM),
+        8,
+    ).reshape(-1, width)
+    gain_one_sum, gain_two_sum = sums[0], sums[1]
+    router_a_sum, router_f_sum = sums[2 : 2 + experts].T, sums[2 + experts :].T
     return (
         layer_output[None],
         input_grad[None],

time: 1570 us -> 1300 us (0.83)
  waiting for transfers between devices: 167 us -> 48.9 us
  blocking collectives: 112 us -> 0 us
  Pallas kernels: 918 us -> 887 us
    psum x1 -> x0, waiting for transfers between devices: 128 us -> none  [placed_weights(): lax.psum((local_gain_one, local_gain_two, local_attn_router, local_ffn_ro...]
    all_gather x2 -> x0, blocking collectives: 112 us -> none  [spread(): whole = lax.all_gather(columns, EVERY, axis=0, tiled=True)]
    psum x1, waiting for transfers between devices: 12 us -> 48.8 us  [placed_weights(): lax.psum(kv_grads.transpose(0, 2, 1, 3).reshape(-1, 2 * QD), 'expert')]
    pallas_call x7 -> x9, Pallas kernels: 879 us -> 848 us  [the longest x4 401 us: scatter_all(): pl.pallas_call(functools.partial(scatter_kernel, count), out_shape=[jax.S...]
    all_to_all x1, waiting for transfers between devices: 27.3 us -> 0.01 us  [placed_weights(): lax.all_to_all(grad_qkv, SHARE, split_axis=0, concat_axis=1, tiled=True)]
  transfers between devices with their start and end apart: 11 -> 7, of which waited for: 3 -> 1; matrix products, arithmetic and copies ran while one was open for 17% -> 20% of each run, Pallas kernels for 59% -> 69%
where the time goes in v2:
time: 1300 us; the launch traced here: 1290 us
  Pallas kernels  887 us (68%)
  matrix products  236 us (18%)
  waiting for transfers between devices  48.9 us (4%)
  starting transfers between devices  40.2 us (3%)
  other arithmetic  37.5 us (3%)
  local copies, waits for them, and re-layouts  28.7 us (2%)
  between operations  16.1 us (1%)
    pallas_call x4, Pallas kernels, scatter_all(): pl.pallas_call(functools.partial(scatter_kernel, count), out_shape=[jax.S...  401 us
    pallas_call x4, Pallas kernels, gather_all(): pl.pallas_call(functools.partial(gather_kernel, count), out_shape=[jax.Sh...  391 us
    pallas_call x1, Pallas kernels, sum_all(): pl.pallas_call(sum_kernel, out_shape=jax.ShapeDtypeStruct(v.shape, v.dtyp...  55.5 us
    psum x1, waiting for transfers between devices, placed_weights(): lax.psum(kv_grads.transpose(0, 2, 1, 3).reshape(-1, 2 * QD), 'expert')  48.8 us
  transfers between devices with their start and end apart: 7, of which 1 were waited for; matrix products, arithmetic and copies ran while one was open for 20% of the time, Pallas kernels for 69%

profile of v2, /device:TPU:8, one launch (start us, length us, event | category | flops | bytes accessed | tf_op | source)
XLA Modules:
  0.0 1294.6 jit_solution(9030526904126034638)
XLA Ops:
  7.2 2.3 copy.52
  9.5 1.6 copy.55
  11.1 2.6 reshape.281
  13.8 1.5 copy.47
  15.8 3.5 pad_maximum_fusion.3
  19.3 6.4 all-to-all-start
  27.9 0.6 pad_maximum_fusion.5.refs_1_
  28.5 128.7 %gather_all.4 = (bf16[32,128,2048]{2,1,0:T(8,128)(2,1)}, f32[32,8,128]{2,1,0:T(8,128)}) custom-call(bf16[128,2048]{1,0:T(8,128)(2,1)} %copy-done.10, f32[8,128]{1,0:T(8,128)} %pad_maximum_fusion.5.refs_1_), custom_call_target="tpu_custom_call" | custom-call | tf_op jit(solution)/shard_map/gather_all/pallas_call | solution.py:636
  157.2 9.8 collective-permute-start
  167.5 1.0 constant_dynamic-slice_fusion.1
  168.7 1.0 fusion.18.refs_0_
  169.6 8.2 all-to-all-start.1
  177.9 19.4 %convolution_convert_fusion.6.qkv_ref = bf16[4096,768]{1,0:T(8,128)(2,1)} fusion(bf16[4096,2048]{1,0:T(8,128)(2,1)} %bitcast.182, bf16[2048,768]{1,0:T(8,128)(2,1)} %bitcast.13), kind=kOutput, calls=%fused_computation.9 | convolution fusion | flops 12888047616 | bytes 26214400 | tf_op jit(solution)/shard_map/dot_general | solution.py:1098
  197.3 15.1 %attend.1 = (bf16[4096,256]{1,0:T(8,128)(2,1)S(1)}, f32[4,2,1024]{2,1,0:T(2,128)S(1)}) custom-call(bf16[4096,768]{1,0:T(8,128)(2,1)} %convolution_convert_fusion.6.qkv_ref), custom_call_target="tpu_custom_call" | custom-call | tf_op jit(solution)/shard_map/attend/pallas_call | solution.py:933
  212.4 8.2 convolution_convert_fusion.1
  220.5 121.2 %scatter_all.4 = bf16[128,2048]{1,0:T(8,128)(2,1)S(1)} custom-call(bf16[32,128,2048]{2,1,0:T(8,128)(2,1)} %bitcast.145), custom_call_target="tpu_custom_call" | custom-call | tf_op jit(solution)/shard_map/scatter_all/pallas_call | solution.py:828
  343.8 106.2 %gather_all.5 = (bf16[32,128,2048]{2,1,0:T(8,128)(2,1)}, f32[32,8,128]{2,1,0:T(8,128)}) custom-call(bf16[128,2048]{1,0:T(8,128)(2,1)} %copy-done.12, f32[8,128]{1,0:T(8,128)} %pad.4.refs_1_), custom_call_target="tpu_custom_call" | custom-call | tf_op jit(solution)/shard_map/gather_all/pallas_call | solution.py:636
  450.0 78.5 %gather_all.6 = bf16[32,128,2048]{2,1,0:T(8,128)(2,1)} custom-call(bf16[128,2048]{1,0:T(8,128)(2,1)} %fusion.18.refs_0_), custom_call_target="tpu_custom_call" | custom-call | tf_op jit(solution)/shard_map/gather_all/pallas_call | solution.py:636
  528.5 12.0 convolution_convert_fusion.7
  540.5 12.1 convolution_convert_fusion.8
  552.6 20.4 %fusion.58 = f32[2304,1408]{0,1:T(8,128)} fusion(bf16[2304,2048]{1,0:T(8,128)(2,1)} %bitcast.146, bf16[1408,2048]{1,0:T(8,128)(2,1)} %bitcast.22), kind=kOutput, calls=%fused_computation.132 | convolution fusion | flops 13287555072 | bytes 28180480 | tf_op jit(solution)/shard_map/dot_general | solution.py:1139
  573.0 13.9 %fusion = (f32[2304]{0:T(1024)S(1)}, bf16[2304,704]{0,1:T(8,128)(2,1)}, f32[2304,704]{0,1:T(8,128)}) fusion(f32[2304,1408]{0,1:T(8,128)} %fusion.58, bf16[2304,2048]{1,0:T(8,128)(2,1)S(1)} %bitcast.149, bf16[704,2048]{1,0:T(8,128)(2,1)} %bitcast.185, bf16[704,2048]{1,0:T(8,128)(2,1)} %collective-permute-done, pred[]{:T(512)S(6)} %or.3), kind=kOutput, calls=%fused_computation.10 | convolution fusion | flops 6659815424 | bytes 37921792 | tf_op jit(solution)/shard_map/dot_general | solution.py:1149
  587.0 0.9 constant_dynamic-slice_fusion
  587.9 1.1 fusion.5
  589.1 12.5 convolution_convert_fusion.11
  601.6 5.0 collective-permute-start.1
  606.7 4.4 multiply_convert_fusion.2
  611.1 13.6 %multiply_convert_fusion = bf16[2304,2048]{1,0:T(8,128)(2,1)} fusion(bf16[2304,704]{0,1:T(8,128)(2,1)} %get-tuple-element.54, f32[2304]{0:T(1024)S(1)} %mul.363, bf16[704,2048]{1,0:T(8,128)(2,1)} %bitcast.186, bf16[704,2048]{1,0:T(8,128)(2,1)} %collective-permute-done, pred[]{:T(512)S(6)} %or.3), kind=kOutput, calls=%fused_computation | convolution fusion | flops 6654656512 | bytes 18457600 | tf_op jit(solution)/shard_map/dot_general | solution.py:1144
  624.6 10.5 convolution_convert_fusion.3.refs_0_
  635.1 85.1 %scatter_all.5 = bf16[128,2048]{1,0:T(8,128)(2,1)S(1)} custom-call(bf16[32,128,2048]{2,1,0:T(8,128)(2,1)} %convolution_convert_fusion.3.refs_0_), custom_call_target="tpu_custom_call" | custom-call | tf_op jit(solution)/shard_map/scatter_all/pallas_call | solution.py:828
  720.2 19.4 %convolution_convert_fusion.4 = bf16[2304,2048]{1,0:T(8,128)(2,1)} fusion(bf16[1408,2048]{1,0:T(8,128)(2,1)} %bitcast.22, bf16[2304,704]{0,1:T(8,128)(2,1)S(1)} %copy-done.17, bf16[2304,704]{0,1:T(8,128)(2,1)S(1)} %get-tuple-element.55), kind=kOutput, calls=%fused_computation.5 | convolution fusion | flops 13305249792 | bytes 21692416 | tf_op jit(solution)/shard_map/dot_general | solution.py:1156
  739.6 10.5 convolution_convert_fusion.2.refs_0_
  750.3 109.8 %scatter_all.6 = (bf16[128,2048]{1,0:T(8,128)(2,1)S(1)}, f32[8,128]{1,0:T(8,128)S(1)}) custom-call(bf16[32,128,2048]{2,1,0:T(8,128)(2,1)} %convolution_convert_fusion.2.refs_0_, f32[32,8,128]{2,1,0:T(8,128)S(1)} %broadcast_multiply_fusion.1.refs_1_), custom_call_target="tpu_custom_call" | custom-call | tf_op jit(solution)/shard_map/scatter_all/pallas_call | solution.py:828
  860.2 1.0 multiply_reduce_fusion
  861.3 1.9 fusion.53
  863.2 77.8 %gather_all.7 = bf16[32,128,2048]{2,1,0:T(8,128)(2,1)} custom-call(bf16[128,2048]{1,0:T(8,128)(2,1)} %get-tuple-element.51.refs_0_), custom_call_target="tpu_custom_call" | custom-call | tf_op jit(solution)/shard_map/gather_all/pallas_call | solution.py:636
  941.0 8.4 convolution_convert_fusion.9.du_ref
  949.4 24.5 %attend_back.1 = (bf16[4096,768]{1,0:T(8,128)(2,1)}, f32[4,2,1024]{2,1,0:T(2,128)S(1)}) custom-call(bf16[4096,768]{1,0:T(8,128)(2,1)} %convolution_convert_fusion.6.qkv_ref, bf16[4096,256]{1,0:T(8,128)(2,1)S(1)} %convolution_convert_fusion.9.du_ref, f32[4,2,1024]{2,1,0:T(2,128)S(1)} %get-tuple-element.40.lse_ref, f32[4,1,1024]{2,1,0:T(1,128)S(1)} %bitcast.141), custom_call_target="tpu_custom_call" | custom-call | tf_op jit(solution)/shard_map/attend_back/pallas_call | solution.py:998
  973.9 20.3 %convolution_convert_fusion.10 = bf16[2048,768]{1,0:T(8,128)(2,1)} fusion(bf16[4096,2048]{1,0:T(8,128)(2,1)} %bitcast.183, bf16[4096,768]{1,0:T(8,128)(2,1)} %get-tuple-element.41), kind=kOutput, calls=%fused_computation.22 | convolution fusion | flops 12886474752 | bytes 26214400 | tf_op jit(solution)/shard_map/dot_general | solution.py:1196
  994.2 4.7 all-to-all-start.2
  999.0 20.1 %convolution_convert_fusion = bf16[4096,2048]{1,0:T(8,128)(2,1)} fusion(bf16[4096,768]{1,0:T(8,128)(2,1)} %get-tuple-element.41, bf16[2048,768]{1,0:T(8,128)(2,1)} %bitcast.13), kind=kOutput, calls=%fused_computation.1 | convolution fusion | flops 12893290496 | bytes 26214400 | tf_op jit(solution)/shard_map/dot_general | solution.py:1193
  1019.1 84.7 %scatter_all.7 = (bf16[128,2048]{1,0:T(8,128)(2,1)S(1)}, f32[8,128]{1,0:T(8,128)S(1)}) custom-call(bf16[32,128,2048]{2,1,0:T(8,128)(2,1)} %bitcast.152, f32[32,8,128]{2,1,0:T(8,128)S(1)} %broadcast_multiply_fusion.refs_1_), custom_call_target="tpu_custom_call" | custom-call | tf_op jit(solution)/shard_map/scatter_all/pallas_call | solution.py:828
  1104.5 18.0 %convolution_convert_fusion.5 = bf16[1408,2048]{1,0:T(8,128)(2,1)} fusion(bf16[2304,2048]{1,0:T(8,128)(2,1)} %bitcast.147, bf16[2304,704]{0,1:T(8,128)(2,1)S(1)} %copy-done.18, bf16[2304,704]{0,1:T(8,128)(2,1)S(1)} %copy-done.16), kind=kOutput, calls=%fused_computation.8 | convolution fusion | flops 13303414784 | bytes 21692416 | tf_op jit(solution)/shard_map/dot_general | solution.py:1163
  1122.5 6.1 all-to-all-start.3
  1128.8 3.2 fusion.16
  1132.0 0.7 reshape.290.v_ref
  1132.7 55.5 %sum_all.1 = f32[160,128]{1,0:T(8,128)} custom-call(f32[160,128]{1,0:T(8,128)} %reshape.290.v_ref), custom_call_target="tpu_custom_call" | custom-call | tf_op jit(solution)/shard_map/sum_all/pallas_call | solution.py:880
  1188.2 0.8 fusion.55
  1189.0 0.6 slice.45
  1189.6 0.6 slice.47
  1190.3 1.3 slice_bitcast_fusion
  1191.6 3.1 fusion.13
  1194.7 11.7 convolution_bitcast_fusion
  1206.4 3.0 slice.52
  1209.4 2.8 reshape.291
  1212.2 2.3 copy.50
  1214.5 2.2 copy.53
  1216.8 8.7 bitcast_convert_fusion
  1225.4 4.7 bitcast_convert_fusion.1
  1230.2 1.4 slice_convert_fusion
  1231.6 1.2 copy.51
  1232.8 1.5 reshape.295
  1234.3 48.8 %all-reduce.3.cloned.1.call-done = bf16[256,4096]{1,0:T(8,128)(2,1)} async-done(((bf16[256,4096]{1,0:T(8,128)(2,1)}), bf16[256,4096]{1,0:T(8,128)(2,1)}) %all-reduce.3.cloned.1.call-update) | async-done | bytes 2097168 | tf_op jit(solution)/shard_map/psum | solution.py:1203
  1283.1 4.1 convert_element_type.188
  (143 shorter events, 6.0 us)
Async XLA Ops:
  7.2 205.2 %copy-start = (bf16[1,256,2048]{2,1,0:T(8,128)(2,1)S(1)}, bf16[1,256,2048]{2,1,0:T(8,128)(2,1)}, u32[]{:S(2)}) copy-start(bf16[1,256,2048]{2,1,0:T(8,128)(2,1)} %param.25) | copy-start | bytes 3145732
  15.8 10.6 copy-start.7
  15.8 11.4 copy-start.23
  15.8 11.5 copy-start.31
  15.8 11.9 copy-start.36
  15.8 12.0 copy-start.35
  19.3 149.3 %copy-start.19 = (bf16[1,128,2048]{2,1,0:T(8,128)(2,1)S(1)}, bf16[1,128,2048]{2,1,0:T(8,128)(2,1)}, u32[]{:S(2)}) copy-start(bf16[1,128,2048]{2,1,0:T(8,128)(2,1)} %param.15) | copy-start | bytes 1572868
  19.3 150.3 %all-to-all-start = ((bf16[256,8,768]{2,0,1:T(8,128)(2,1)}), bf16[256,8,768]{2,0,1:T(8,128)(2,1)}, u32[]{:S(2)}, u32[]{:S(2)}) async-start(bf16[256,8,768]{2,0,1:T(8,128)(2,1)} %pad_maximum_fusion.3), calls=%async_computation | async-start | bytes 6291456 | tf_op jit(solution)/shard_map/all_to_all | solution.py:1074
  27.1 0.6 copy-start.37
  27.3 1.1 copy-start.10
  27.8 315.3 %copy-start.33 = (f32[128]{0:T(128)}, f32[128]{0:T(128)S(1)}, u32[]{:S(2)}) copy-start(f32[128]{0:T(128)S(1)} %compare_convert_fusion.1) | copy-start | bytes 1540
  27.9 139.7 %copy-start.25 = (f32[128,4]{0,1:T(4,128)}, f32[128,4]{0,1:T(4,128)S(1)}, u32[]{:S(2)}) copy-start(f32[128,4]{0,1:T(4,128)S(1)} %select_reduce_fusion.2) | copy-start | bytes 6148
  157.2 415.8 %collective-permute-start = (bf16[704,2048]{1,0:T(8,128)(2,1)}, bf16[704,2048]{1,0:T(8,128)(2,1)}, u32[]{:S(2)}, u32[]{:S(2)}) collective-permute-start(bf16[704,2048]{1,0:T(8,128)(2,1)} %bitcast.184), channel_id=1, source_target_pairs={{1,4},{2,1},{3,5},{4,2},{5,6},{6,3},{9,12},{10,9},{11,13},{12,10},... | collective-permute-start | bytes 8650760 | tf_op jit(solution)/shard_map/ppermute | solution.py:1095
  169.6 383.0 %all-to-all-start.1 = ((bf16[2,704,2048]{2,1,0:T(8,128)(2,1)}), bf16[2,704,2048]{2,1,0:T(8,128)(2,1)}, u32[]{:S(2)}, u32[]{:S(2)}) async-start(bf16[2,704,2048]{2,1,0:T(8,128)(2,1)} %bitcast.159), calls=%async_computation.1 | async-start | bytes 11534336 | tf_op jit(solution)/shard_map/all_to_all | solution.py:1091
  212.3 8.2 copy-start.1
  220.5 121.2 %copy-start.8 = (bf16[1,128,2048]{2,1,0:T(8,128)(2,1)S(1)}, bf16[1,128,2048]{2,1,0:T(8,128)(2,1)}, u32[]{:S(2)}) copy-start(bf16[1,128,2048]{2,1,0:T(8,128)(2,1)} %param.14) | copy-start | bytes 1572868
  220.5 122.0 %copy-start.21 = (f32[2048]{0:T(1024)S(1)}, f32[2048]{0:T(1024)}, u32[]{:S(2)}) copy-start(f32[2048]{0:T(1024)} %param.20) | copy-start | bytes 24580
  220.5 122.2 %copy-start.29 = (bf16[2048,4]{0,1:T(4,128)(2,1)S(1)}, bf16[2048,4]{0,1:T(4,128)(2,1)}, u32[]{:S(2)}) copy-start(bf16[2048,4]{0,1:T(4,128)(2,1)} %param.22) | copy-start | bytes 49156
  341.7 0.8 copy-start.3
  342.5 186.0 %copy-start.40 = (f32[128]{0:T(128)}, f32[128]{0:T(128)S(1)}, u32[]{:S(2)}) copy-start(f32[128]{0:T(128)S(1)} %get-tuple-element.67) | copy-start | bytes 1540
  342.8 1.0 copy-start.12
  343.1 185.4 %copy-start.27 = (f32[128,4]{0,1:T(4,128)}, f32[128,4]{0,1:T(4,128)S(1)}, u32[]{:S(2)}) copy-start(f32[128,4]{0,1:T(4,128)S(1)} %select_reduce_fusion) | copy-start | bytes 6148
  552.6 20.4 %copy-start.6 = (bf16[32,72,2048]{2,1,0:T(8,128)(2,1)S(1)}, bf16[32,72,2048]{2,1,0:T(8,128)(2,1)}, u32[]{:S(2)}) copy-start(bf16[32,72,2048]{2,1,0:T(8,128)(2,1)} %convolution_convert_fusion.7) | copy-start | bytes 28311556
  589.1 17.6 %slice-start = ((s8[12976128]{0:T(1024)(128)(4,1)}), s8[4194304]{0:T(1024)(128)(4,1)S(1)}, s32[]{:S(2)}) async-start(s8[12976128]{0:T(1024)(128)(4,1)} %bitcast.153), calls=%async_computation.5 | async-start | bytes 8388608
  589.1 17.6 %slice-start.1 = ((s8[12976128]{0:T(1024)(128)(4,1)}), s8[4194304]{0:T(1024)(128)(4,1)S(1)}, s32[]{:S(2)}) async-start(s8[12976128]{0:T(1024)(128)(4,1)} %bitcast.153), calls=%async_computation.6 | async-start | bytes 8388608
  589.1 17.6 %slice-start.2 = ((s8[12976128]{0:T(1024)(128)(4,1)}), s8[4194304]{0:T(1024)(128)(4,1)S(1)}, s32[]{:S(2)}) async-start(s8[12976128]{0:T(1024)(128)(4,1)} %bitcast.153), calls=%async_computation.7 | async-start | bytes 8388608
  589.1 17.6 %slice-start.3 = ((s8[12976128]{0:T(1024)(128)(4,1)}), s8[393216]{0:T(1024)(128)(4,1)S(1)}, s32[]{:S(2)}) async-start(s8[12976128]{0:T(1024)(128)(4,1)} %bitcast.153), calls=%async_computation.8 | async-start | bytes 786432
  589.1 17.6 %copy-start.14 = (f32[2304,704]{0,1:T(8,128)S(1)}, f32[2304,704]{0,1:T(8,128)}, u32[]{:S(2)}) copy-start(f32[2304,704]{0,1:T(8,128)} %get-tuple-element.68) | copy-start | bytes 19464196
  601.6 623.8 %collective-permute-start.1 = (bf16[704,2048]{1,0:T(8,128)(2,1)}, bf16[704,2048]{1,0:T(8,128)(2,1)}, u32[]{:S(2)}, u32[]{:S(2)}) collective-permute-start(bf16[704,2048]{1,0:T(8,128)(2,1)} %convolution_convert_fusion.11), channel_id=1, source_target_pairs={{4,1},{1,2},{5,3},{2,4},{6,5},{3,6},{12,9},{9,10},{13,11},{10,12},... | collective-permute-start | bytes 8650760 | tf_op jit(solution)/shard_map/ppermute | solution.py:1169
  611.1 109.2 %copy-start.15 = (bf16[2304,704]{0,1:T(8,128)(2,1)}, bf16[2304,704]{0,1:T(8,128)(2,1)S(1)}, u32[]{:S(2)}) copy-start(bf16[2304,704]{0,1:T(8,128)(2,1)S(1)} %get-tuple-element.55) | copy-start | bytes 9732100
  635.1 85.1 %copy-start.17 = (bf16[2304,704]{0,1:T(8,128)(2,1)S(1)}, bf16[2304,704]{0,1:T(8,128)(2,1)}, u32[]{:S(2)}) copy-start(bf16[2304,704]{0,1:T(8,128)(2,1)} %get-tuple-element.56) | copy-start | bytes 9732100
  739.6 10.5 copy-start.39
  750.2 109.9 %copy-start.28 = (f32[128,4]{0,1:T(4,128)S(1)}, f32[128,4]{0,1:T(4,128)}, u32[]{:S(2)}) copy-start(f32[128,4]{0,1:T(4,128)} %copy-done.27) | copy-start | bytes 6148
  750.2 110.0 %copy-start.4 = (bf16[128,2048]{1,0:T(8,128)(2,1)S(1)}, bf16[128,2048]{1,0:T(8,128)(2,1)}, u32[]{:S(2)}) copy-start(bf16[128,2048]{1,0:T(8,128)(2,1)} %copy-done.3) | copy-start | bytes 1572868
  750.2 110.0 %copy-start.9 = (bf16[1,128,2048]{2,1,0:T(8,128)(2,1)S(1)}, bf16[1,128,2048]{2,1,0:T(8,128)(2,1)}, u32[]{:S(2)}) copy-start(bf16[1,128,2048]{2,1,0:T(8,128)(2,1)} %param.14) | copy-start | bytes 1572868
  750.2 110.0 %copy-start.22 = (f32[2048]{0:T(1024)S(1)}, f32[2048]{0:T(1024)}, u32[]{:S(2)}) copy-start(f32[2048]{0:T(1024)} %param.20) | copy-start | bytes 24580
  750.2 110.0 %copy-start.30 = (bf16[2048,4]{0,1:T(4,128)(2,1)S(1)}, bf16[2048,4]{0,1:T(4,128)(2,1)}, u32[]{:S(2)}) copy-start(bf16[2048,4]{0,1:T(4,128)(2,1)} %param.22) | copy-start | bytes 49156
  750.2 109.9 %copy-start.41 = (f32[128]{0:T(128)S(1)}, f32[128]{0:T(128)}, u32[]{:S(2)}) copy-start(f32[128]{0:T(128)} %copy-done.40) | copy-start | bytes 1540
  750.3 111.0 %copy-start.20 = (bf16[1,128,2048]{2,1,0:T(8,128)(2,1)S(1)}, bf16[1,128,2048]{2,1,0:T(8,128)(2,1)}, u32[]{:S(2)}) copy-start(bf16[1,128,2048]{2,1,0:T(8,128)(2,1)} %param.15) | copy-start | bytes 1572868
  750.3 111.0 %copy-start.34 = (f32[128]{0:T(128)S(1)}, f32[128]{0:T(128)}, u32[]{:S(2)}) copy-start(f32[128]{0:T(128)} %copy-done.33) | copy-start | bytes 1540
  750.3 111.0 %copy-start.43 = (f32[128]{0:T(128)S(1)}, f32[128]{0:T(128)}, u32[]{:S(2)}) copy-start(f32[128]{0:T(128)} %get-tuple-element.66) | copy-start | bytes 1540
  994.2 128.3 %all-to-all-start.2 = ((bf16[8,256,768]{2,1,0:T(8,128)(2,1)}), bf16[8,256,768]{2,1,0:T(8,128)(2,1)}, u32[]{:S(2)}, u32[]{:S(2)}) async-start(bf16[8,256,768]{2,1,0:T(8,128)(2,1)} %bitcast.162), calls=%async_computation.2 | async-start | bytes 6291456 | tf_op jit(solution)/shard_map/all_to_all | solution.py:1199
  1019.1 84.8 %copy-start.26 = (f32[128,4]{0,1:T(4,128)S(1)}, f32[128,4]{0,1:T(4,128)}, u32[]{:S(2)}) copy-start(f32[128,4]{0,1:T(4,128)} %copy-done.25) | copy-start | bytes 6148
  1019.1 84.8 %copy-start.13 = (bf16[128,2048]{1,0:T(8,128)(2,1)S(1)}, bf16[128,2048]{1,0:T(8,128)(2,1)}, u32[]{:S(2)}) copy-start(bf16[128,2048]{1,0:T(8,128)(2,1)} %copy-done.12) | copy-start | bytes 1572868
  1019.1 85.1 %copy-start.11 = (bf16[128,2048]{1,0:T(8,128)(2,1)S(1)}, bf16[128,2048]{1,0:T(8,128)(2,1)}, u32[]{:S(2)}) copy-start(bf16[128,2048]{1,0:T(8,128)(2,1)} %copy-done.10) | copy-start | bytes 1572868
  1019.1 85.4 %copy-start.16 = (bf16[2304,704]{0,1:T(8,128)(2,1)S(1)}, bf16[2304,704]{0,1:T(8,128)(2,1)}, u32[]{:S(2)}) copy-start(bf16[2304,704]{0,1:T(8,128)(2,1)} %copy-done.15) | copy-start | bytes 9732100
  1019.1 85.4 %copy-start.18 = (bf16[2304,704]{0,1:T(8,128)(2,1)S(1)}, bf16[2304,704]{0,1:T(8,128)(2,1)}, u32[]{:S(2)}) copy-start(bf16[2304,704]{0,1:T(8,128)(2,1)} %get-tuple-element.56) | copy-start | bytes 9732100
  1103.8 18.7 %copy-start.5 = (bf16[128,2048]{1,0:T(8,128)(2,1)}, bf16[128,2048]{1,0:T(8,128)(2,1)S(1)}, u32[]{:S(2)}) copy-start(bf16[128,2048]{1,0:T(8,128)(2,1)S(1)} %get-tuple-element.43) | copy-start | bytes 1572868
  1122.5 6.2 copy-start.24
  1122.5 6.3 copy-start.32
  1122.5 6.3 copy-start.38
  1122.5 69.0 %copy-start.42 = (f32[128]{0:T(128)S(1)}, f32[128]{0:T(128)}, u32[]{:S(2)}) copy-start(f32[128]{0:T(128)} %get-tuple-element.64) | copy-start | bytes 1540
  1122.5 94.2 %all-to-all-start.3 = ((bf16[2,704,2048]{2,1,0:T(8,128)(2,1)}), bf16[2,704,2048]{2,1,0:T(8,128)(2,1)}, u32[]{:S(2)}, u32[]{:S(2)}) async-start(bf16[2,704,2048]{2,1,0:T(8,128)(2,1)} %bitcast.160), calls=%async_computation.3 | async-start | bytes 11534336 | tf_op jit(solution)/shard_map/all_to_all | solution.py:1166
  1128.7 66.0 %copy-start.2 = (bf16[4096,256]{1,0:T(8,128)(2,1)S(1)}, bf16[4096,256]{1,0:T(8,128)(2,1)}, u32[]{:S(2)}) copy-start(bf16[4096,256]{1,0:T(8,128)(2,1)} %copy-done.1) | copy-start | bytes 6291460
  1128.7 154.4 %all-reduce.3.cloned.1.call-start = ((), (), s32[]{:S(2)}) async-start(), calls=%async_computation.4 | async-start | bytes 4194304 | tf_op jit(solution)/shard_map/psum | solution.py:1203
Sparse Core Ops, SparseCore 0:
  1216.9 66.2 all-reduce.2
